TPU v7x, 32 devices: a whole 2x2x4 slice. The times are simulated.
32 devices in a mesh: dp: 16 (over z, y, core), tensor: 2 (over x).
Axes of the slice: x: 2, y: 2, z: 4, core: 2. Of those that a mesh axis runs over, the one named last changes fastest.
Arguments:
- activations: bfloat16 [32768, 1024], P(('dp', 'tensor')), may hold values from -6 to 6
- gradients: bfloat16 [32768, 5472], P('dp', 'tensor'), may hold values from -6 to 6
- act_history: float32 [2, 16, 1024], P('tensor'), may hold values from 0.1 to 4
- grad_history: float32 [16, 5472], P(None, 'tensor'), may hold values from 0.1 to 4
- owner_rank: int32 [1024], replicated, may hold values from 0 to 1
- history_slot: int32 [6496], replicated, may hold values from 0 to 15
Outputs:
- weight_grad: float32 [1024, 5472], P('dp', 'tensor')
- act_history_out: float32 [2, 16, 1024], P('tensor')
- grad_history_out: float32 [16, 5472], P(None, 'tensor')
All inputs are finite; a program needn't handle non-finite values.
Results may differ from a plain program's by a relative error of at most 0.0042.
Values may be sent and summed in bfloat16 or wider, within the bound.
A program may use at most 64 MiB of HBM per device.

v0:
```python
import functools
import math

import jax
import jax.numpy as jnp
from jax import lax
from jax.experimental import pallas as pl
from jax.experimental.pallas import tpu as pltpu
from jax.sharding import PartitionSpec as P

QUANT_LIMIT = 448.0
SCALE_FLOOR = 0.25
CORES = 2
ROWS_Y = 2
LANES = 128
SUBLANES = 16
COL_TILE = 1408
MESH = pl.DeviceIdType.MESH


def quantize(values, scale):
    scaled = values.astype(jnp.float32) * scale
    return jnp.clip(scaled, -QUANT_LIMIT, QUANT_LIMIT).astype(jnp.bfloat16)


def place_peaks(history, peaks, slots):
    rows = lax.broadcasted_iota(jnp.int32, history.shape, 0)
    return jnp.where(rows == slots[None, :], peaks[None, :], history)


def col_tiles(width):
    return [(start, min(COL_TILE, width - start)) for start in range(0, width, COL_TILE)]


def fused_kernel(
    dp, tensor,
    act_hbm, grad_hbm, act_hist_ref, grad_hist_ref, owner_ref, slot_ref,
    weight_ref, act_hist_out, grad_hist_out,
    act_own, act_got, hist_got, gq, part, core_got, y_out, y_got, z_out, z_got,
    lhs, peaks, act_peaks, act_scale, grad_scale, scale_down, peak_down, row_undo, current_hist,
    load_sem, grad_sem, hist_send, hist_recv, x_send, x_recv, core_send, core_recv,
    y_send, y_recv, z_send, z_recv, pk_send, pk_recv, ap_send, ap_recv,
):
    me = lax.axis_index("dp")
    mt = lax.axis_index("tensor")
    core = lax.rem(me, CORES)
    chip = lax.div(me, CORES)
    yy = lax.rem(chip, ROWS_Y)
    zz = lax.div(chip, ROWS_Y)
    depth = dp // (CORES * ROWS_Y)
    tokens, width = act_hbm.shape
    cols, rows = grad_hbm.shape
    block = width // dp
    pair = block * CORES
    load_cols = cols // grad_sem.shape[0]
    padded = grad_scale.shape[1]

    def dp_index(z, y, c):
        return (z * ROWS_Y + y) * CORES + c

    sibling = dp_index(zz, yy, 1 - core)
    y_peer = dp_index(zz, 1 - yy, core)

    def grad_load(i):
        at = pl.ds(pl.multiple_of(i * load_cols, SUBLANES), load_cols)
        return pltpu.make_async_copy(grad_hbm.at[at], gq.at[at], grad_sem.at[i])

    def start_load(i, carry):
        grad_load(i).start()
        return carry

    act_load = pltpu.make_async_copy(act_hbm, act_own, load_sem)
    act_load.start()
    lax.fori_loop(0, grad_sem.shape[0], start_load, 0)

    barrier = pltpu.get_barrier_semaphore()
    for t in range(1, tensor):
        pl.semaphore_signal(
            barrier, inc=1, device_id={"tensor": lax.rem(mt + t, tensor)}, device_id_type=MESH
        )

    def greet(k, carry):
        pl.semaphore_signal(
            barrier, inc=1, device_id={"dp": lax.rem(me + k, dp)}, device_id_type=MESH
        )
        return carry

    lax.fori_loop(1, dp, greet, 0)
    pl.semaphore_wait(barrier, dp - 1 + tensor - 1)

    def target_z(u):
        return lax.rem(zz + 1 + u, depth)

    def block_cols(u, k):
        y = yy * k + (1 - yy) * (1 - k)
        return pl.ds(pl.multiple_of((target_z(u) * ROWS_Y + y) * pair, LANES), pair)

    def line_cols(u):
        return pl.ds(pl.multiple_of(target_z(u) * (ROWS_Y * pair), LANES), ROWS_Y * pair)

    def hist_copy(t):
        return pltpu.make_async_remote_copy(
            src_ref=act_hist_ref.at[0], dst_ref=hist_got.at[t - 1],
            send_sem=hist_send.at[t - 1], recv_sem=hist_recv.at[t - 1],
            device_id={"tensor": lax.rem(mt + t, tensor)}, device_id_type=MESH,
        )

    def x_copy(t, u, k):
        at = block_cols(u, k)
        return pltpu.make_async_remote_copy(
            src_ref=act_hbm.at[:, at], dst_ref=act_got.at[t - 1, :, at],
            send_sem=x_send.at[t - 1, u * 2 + k], recv_sem=x_recv.at[t - 1, u * 2 + k],
            device_id={"tensor": lax.rem(mt + t, tensor)}, device_id_type=MESH,
        )

    def side(k):
        return yy * k + (1 - yy) * (1 - k)

    def half_rows(k, c):
        return pl.ds(pl.multiple_of(side(k) * pair + c * block, block), block)

    def core_copy(u, k):
        s = u * 2 + k
        return pltpu.make_async_remote_copy(
            src_ref=part.at[u, half_rows(k, 1 - core)], dst_ref=core_got.at[s],
            send_sem=core_send.at[s], recv_sem=core_recv.at[s],
            device_id={"dp": sibling}, device_id_type=MESH,
        )

    def y_copy(u):
        return pltpu.make_async_remote_copy(
            src_ref=y_out.at[u], dst_ref=y_got.at[u],
            send_sem=y_send.at[u], recv_sem=y_recv.at[u],
            device_id={"dp": y_peer}, device_id_type=MESH,
        )

    def z_copy(u):
        return pltpu.make_async_remote_copy(
            src_ref=z_out.at[u], dst_ref=z_got.at[u],
            send_sem=z_send.at[u], recv_sem=z_recv.at[u],
            device_id={"dp": dp_index(target_z(u), yy, core)}, device_id_type=MESH,
        )

    def peak_copy(k):
        return pltpu.make_async_remote_copy(
            src_ref=peaks.at[0], dst_ref=peaks.at[k],
            send_sem=pk_send.at[k - 1], recv_sem=pk_recv.at[k - 1],
            device_id={"dp": lax.rem(me + k, dp)}, device_id_type=MESH,
        )

    def act_peak_copy(t):
        return pltpu.make_async_remote_copy(
            src_ref=act_peaks.at[0], dst_ref=act_peaks.at[t],
            send_sem=ap_send.at[t - 1], recv_sem=ap_recv.at[t - 1],
            device_id={"tensor": lax.rem(mt + t, tensor)}, device_id_type=MESH,
        )

    for t in range(1, tensor):
        hist_copy(t).start()

    def send_x(u, k):
        for t in range(1, tensor):
            x_copy(t, u, k).start()

    def send_pair(u, carry):
        send_x(u + 1, 0)
        send_x(u, 1)
        return carry

    send_x(0, 0)
    lax.fori_loop(0, depth - 1, send_pair, 0)
    send_x(depth - 1, 1)

    grad_scale[:, padded - LANES:] = jnp.ones((1, LANES), jnp.float32)
    grad_scale[:, :cols] = QUANT_LIMIT / jnp.maximum(
        jnp.max(grad_hist_ref[...], axis=0, keepdims=True), SCALE_FLOOR
    )
    peak_down[padded - LANES:, :] = jnp.zeros((LANES, LANES), jnp.float32)

    def turn_scale(j, carry):
        at = pl.ds(pl.multiple_of(j * LANES, LANES), LANES)
        scale_down[at, :] = jnp.transpose(jnp.broadcast_to(grad_scale[:, at], (LANES, LANES)))
        return carry

    lax.fori_loop(0, padded // LANES, turn_scale, 0)

    act_load.wait()
    step_rows = min(64, tokens)
    for start, size in col_tiles(width):
        def peak_rows(r, top, start=start, size=size):
            at = pl.ds(pl.multiple_of(r * step_rows, step_rows), step_rows)
            mag = jnp.abs(act_own[at, start:start + size])
            return jnp.maximum(top, jnp.max(mag.reshape(step_rows // 16, 16, size), axis=0))

        top = lax.fori_loop(
            0, tokens // step_rows, peak_rows, jnp.zeros((16, size), jnp.bfloat16)
        )
        peaks[0, :, start:start + size] = jnp.max(
            top.astype(jnp.float32), axis=0, keepdims=True
        )
    def grad_chunk(i, carry):
        grad_load(i).wait()

        def quant_cols(j, inner):
            at = pl.ds(pl.multiple_of(i * load_cols + j * SUBLANES, SUBLANES), SUBLANES)
            scale = scale_down[at, :]
            top = jnp.zeros((SUBLANES, LANES), jnp.bfloat16)
            for start in range(0, rows, LANES):
                raw = gq[at, start:start + LANES]
                top = jnp.maximum(top, jnp.abs(raw))
                gq[at, start:start + LANES] = quantize(raw, scale)
            peak_down[at, :] = top.astype(jnp.float32)
            return inner

        return lax.fori_loop(0, load_cols // SUBLANES, quant_cols, carry)

    lax.fori_loop(0, grad_sem.shape[0], grad_chunk, 0)

    def turn_peak(j, carry):
        at = pl.ds(pl.multiple_of(j * LANES, LANES), LANES)
        turned = jnp.transpose(peak_down[at, :])
        here = pl.ds(pl.multiple_of(width + j * LANES, LANES), LANES)
        peaks[0, :, here] = jnp.max(turned, axis=0, keepdims=True)
        return carry

    lax.fori_loop(0, padded // LANES, turn_peak, 0)

    def start_peak(k, carry):
        peak_copy(k).start()
        return carry

    lax.fori_loop(1, dp, start_peak, 0)

    owner = owner_ref[...]
    current = jnp.where(owner == mt, act_hist_ref[0], 0.0)
    for t in range(1, tensor):
        hist_copy(t).wait()
        source = lax.rem(mt + tensor - t, tensor)
        current = jnp.where(owner == source, hist_got[t - 1], current)
    current_hist[...] = current
    act_scale[...] = QUANT_LIMIT / jnp.maximum(
        jnp.max(current, axis=0, keepdims=True), SCALE_FLOOR
    )

    def load_lhs(read, at):
        return jnp.transpose(quantize(read, act_scale[:, at]))

    def multiply(put, left, source):
        at = pl.ds(pl.multiple_of(source * tokens, tokens), tokens)
        full = cols // COL_TILE

        def one(start, size):
            here = pl.ds(start, size)
            put(here, lax.dot_general(
                left[...], gq[here, at], (((1,), (1,)), ((), ())),
                preferred_element_type=jnp.float32,
            ))

        def tile(j, carry):
            one(pl.multiple_of(j * COL_TILE, COL_TILE), COL_TILE)
            return carry

        lax.fori_loop(0, full, tile, 0)
        if cols % COL_TILE:
            one(full * COL_TILE, cols % COL_TILE)

    def own_product(u):
        at = line_cols(u)
        lhs[...] = load_lhs(act_own[:, at], at)

        def put(here, term):
            part[u, :, here] = term

        multiply(put, lhs, mt)

    def got_product(u, k):
        at = block_cols(u, k)
        down = pl.ds(pl.multiple_of(side(k) * pair, pair), pair)

        def put(here, term):
            part[u, down, here] += term

        for t in range(1, tensor):
            x_copy(t, u, k).wait_recv()
            lhs[:pair, :] = load_lhs(act_got[t - 1, :, at], at)
            multiply(put, lhs.at[:pair], lax.rem(mt + tensor - t, tensor))
        core_copy(u, k).start()

    def core_sum(u, k):
        core_copy(u, k).wait_recv()
        return part[u, half_rows(k, core), :] + core_got[u * 2 + k]

    def send_y(u):
        y_out[u] = core_sum(u, 0).astype(jnp.bfloat16)
        y_copy(u).start()

    def line_sum(u):
        y_copy(u).wait_recv()
        return core_sum(u, 1) + y_got[u].astype(jnp.float32)

    own_product(0)
    got_product(0, 0)
    if depth > 1:
        own_product(1)
    send_y(0)

    def unit(u, carry):
        got_product(u + 1, 0)

        @pl.when(u + 2 < depth)
        def _():
            own_product(u + 2)

        send_y(u + 1)
        got_product(u, 1)
        z_out[u] = line_sum(u).astype(jnp.bfloat16)
        z_copy(u).start()
        return carry

    lax.fori_loop(0, depth - 1, unit, 0)

    def wait_peak(k, carry):
        peak_copy(k).wait()
        return carry

    lax.fori_loop(1, dp, wait_peak, 0)
    tops = jnp.max(peaks[...], axis=0)
    act_peaks[0] = tops[:, :width]
    for t in range(1, tensor):
        act_peak_copy(t).start()
    hist_row = lax.broadcasted_iota(jnp.int32, grad_hist_ref.shape, 0)
    grad_slots = slot_ref[:, width:width + cols]
    for t in range(1, tensor):
        first = width + t * cols
        grad_slots = jnp.where(mt == t, slot_ref[:, first:first + cols], grad_slots)
    grad_hist_out[...] = jnp.where(
        hist_row == grad_slots, tops[:, width:width + cols], grad_hist_ref[...]
    )

    picks = lax.broadcasted_iota(jnp.int32, (block, width), 1) == (
        lax.broadcasted_iota(jnp.int32, (block, width), 0) + me * block
    )
    row_scale = jnp.sum(jnp.where(picks, act_scale[...], 0.0), axis=1, keepdims=True)
    row_undo[...] = jnp.broadcast_to(1.0 / row_scale, row_undo.shape)
    factor = 1.0 / math.sqrt(rows * dp)
    grad_scale[...] = factor / grad_scale[...]

    for t in range(1, tensor):
        act_peak_copy(t).wait()
    hist_row = lax.broadcasted_iota(jnp.int32, current_hist.shape, 0)
    act_hist_out[0] = jnp.where(
        hist_row == slot_ref[:, :width], jnp.max(act_peaks[...], axis=0), current_hist[...]
    )

    got_product(depth - 1, 1)
    total = line_sum(depth - 1)
    for u in range(depth - 1):
        z_copy(u).wait_recv()
        total = total + z_got[u].astype(jnp.float32)
    weight_ref[...] = total * row_undo[:, :1] * grad_scale[:, :cols]

    def finish(u, carry):
        for k in range(2):
            for t in range(1, tensor):
                x_copy(t, u, k).wait_send()
            core_copy(u, k).wait_send()
        y_copy(u).wait_send()
        return carry

    lax.fori_loop(0, depth, finish, 0)

    def finish_z(u, carry):
        z_copy(u).wait_send()
        return carry

    lax.fori_loop(0, depth - 1, finish_z, 0)


def fused_outputs(activations, gradients, act_history, grad_history, owner_rank, history_slot):
    dp, tensor = lax.axis_size("dp"), lax.axis_size("tensor")
    tokens, width = activations.shape
    rows, cols = gradients.shape
    hist = act_history.shape[1]
    depth = dp // (CORES * ROWS_Y)
    steps = depth * ROWS_Y
    block = width // dp
    loads = max(n for n in range(1, 13) if (cols // SUBLANES) % n == 0)
    padded = pl.cdiv(cols, LANES) * LANES
    dma = pltpu.SemaphoreType.DMA
    vmem = pl.BlockSpec(memory_space=pltpu.VMEM)
    hbm = pl.BlockSpec(memory_space=pl.ANY)
    f32, bf16 = jnp.float32, jnp.bfloat16
    others = tensor - 1
    return pl.pallas_call(
        functools.partial(fused_kernel, dp, tensor),
        out_shape=(
            jax.ShapeDtypeStruct((block, cols), f32),
            jax.ShapeDtypeStruct((1, hist, width), f32),
            jax.ShapeDtypeStruct((hist, cols), f32),
        ),
        in_specs=[hbm, hbm, vmem, vmem, vmem, vmem],
        out_specs=(vmem, vmem, vmem),
        scratch_shapes=[
            pltpu.VMEM((tokens, width), bf16),
            pltpu.VMEM((others, tokens, width), bf16),
            pltpu.VMEM((others, hist, width), f32),
            pltpu.VMEM((cols, rows), bf16),
            pltpu.VMEM((depth, ROWS_Y * CORES * block, cols), f32),
            pltpu.VMEM((steps, block, cols), f32),
            pltpu.VMEM((depth, block, cols), bf16),
            pltpu.VMEM((depth, block, cols), bf16),
            pltpu.VMEM((depth, block, cols), bf16),
            pltpu.VMEM((depth, block, cols), bf16),
            pltpu.VMEM((ROWS_Y * CORES * block, tokens), bf16),
            pltpu.VMEM((dp, 1, width + padded), f32),
            pltpu.VMEM((tensor, 1, width), f32),
            pltpu.VMEM((1, width), f32),
            pltpu.VMEM((1, padded), f32),
            pltpu.VMEM((padded, LANES), f32),
            pltpu.VMEM((padded, LANES), f32),
            pltpu.VMEM((block, LANES), f32),
            pltpu.VMEM((hist, width), f32),
            dma, dma((loads,)), dma((others,)), dma((others,)),
            dma((others, steps)), dma((others, steps)), dma((steps,)), dma((steps,)),
            dma((depth,)), dma((depth,)), dma((depth,)), dma((depth,)),
            dma((dp - 1,)), dma((dp - 1,)), dma((others,)), dma((others,)),
        ],
        compiler_params=pltpu.CompilerParams(
            collective_id=0, has_side_effects=True, vmem_limit_bytes=60 * 1024 * 1024
        ),
    )(
        activations, gradients.T, act_history, grad_history,
        owner_rank[None, :], history_slot[None, :],
    )


def hand_over_kernel(*refs):
    half = len(refs) // 2
    for source, target in zip(refs[:half], refs[half:]):
        target[...] = source[...]


def hand_over(*results):
    vmem = pl.BlockSpec(memory_space=pltpu.VMEM)
    return pl.pallas_call(
        hand_over_kernel,
        out_shape=tuple(jax.ShapeDtypeStruct(r.shape, r.dtype) for r in results),
        in_specs=[vmem] * len(results),
        out_specs=(vmem,) * len(results),
        compiler_params=pltpu.CompilerParams(vmem_limit_bytes=4 * 1024 * 1024),
    )(*results)


def gathered_sums(activations, gradients, act_history, grad_history, owner_rank):
    my_rank = lax.axis_index("tensor")
    held = jnp.where(owner_rank[None, :] == my_rank, act_history[0], jnp.float32(0.0))
    current = lax.psum(held, "tensor")
    act_scale = QUANT_LIMIT / jnp.maximum(jnp.max(current, axis=0), SCALE_FLOOR)
    grad_scale = QUANT_LIMIT / jnp.maximum(jnp.max(grad_history, axis=0), SCALE_FLOOR)
    gathered_rows = lax.all_gather(quantize(activations, act_scale), "tensor", axis=0, tiled=True)
    summed = lax.psum_scatter(
        lax.dot_general(
            gathered_rows, quantize(gradients, grad_scale), (((0,), (0,)), ((), ())),
            preferred_element_type=jnp.float32,
        ),
        "dp", scatter_dimension=0, tiled=True,
    )
    act_peak = lax.pmax(jnp.max(jnp.abs(activations), axis=0).astype(jnp.float32), ("dp", "tensor"))
    grad_peak = lax.pmax(jnp.max(jnp.abs(gradients), axis=0).astype(jnp.float32), "dp")
    return summed, current, act_peak[None, :], grad_peak[None, :]


def body(activations, gradients, act_history, grad_history, owner_rank, history_slot):
    dp = lax.axis_size("dp")
    model_width = act_history.shape[2]
    column_total = gradients.shape[1]
    row_count = model_width // dp
    fits = dp % (CORES * ROWS_Y) == 0 and (row_count * CORES) % LANES == 0
    fits = fits and column_total % SUBLANES == 0
    if fits:
        return hand_over(*fused_outputs(
            activations, gradients, act_history, grad_history, owner_rank, history_slot
        ))
    act_slots = history_slot[:model_width]
    grad_slots = lax.dynamic_slice_in_dim(
        history_slot, model_width + lax.axis_index("tensor") * column_total, column_total, 0
    )
    summed, current, act_peak, grad_peak = gathered_sums(
        activations, gradients, act_history, grad_history, owner_rank
    )
    act_scale = QUANT_LIMIT / jnp.maximum(jnp.max(current, axis=0), SCALE_FLOOR)
    grad_scale = QUANT_LIMIT / jnp.maximum(jnp.max(grad_history, axis=0), SCALE_FLOOR)
    grad_factor = 1.0 / math.sqrt(gradients.shape[0] * dp)
    row_base = lax.axis_index("dp") * row_count
    row_scale = lax.dynamic_slice_in_dim(act_scale, row_base, row_count, 0)
    weight_grad = summed / (row_scale[:, None] * grad_scale[None, :]) * grad_factor
    act_history_out = place_peaks(current, act_peak[0], act_slots)[None]
    grad_history_out = place_peaks(grad_history, grad_peak[0], grad_slots)
    return (weight_grad, act_history_out, grad_history_out)


def solution(mesh):
    placed = (
        P(("dp", "tensor"), None),
        P("dp", "tensor"),
        P("tensor", None, None),
        P(None, "tensor"),
        P(),
        P(),
    )
    return jax.shard_map(
        body,
        mesh=mesh,
        in_specs=placed,
        out_specs=(P("dp", "tensor"), P("tensor", None, None), P(None, "tensor")),
        check_vma=False,
    )
```

profile of v0, /device:TPU:0, one launch (start us, length us, event | category | flops | bytes accessed | tf_op | source)
XLA Modules:
  0.0 75.4 jit_solution(1421992673802967529)
XLA Ops:
  0.6 1.4 %broadcast_in_dim.7.slot_ref = s32[1,6496]{1,0:T(1,128)} reshape(s32[6496]{0:T(1024)} %param.11) | data formatting | bytes 51968 | tf_op jit(solution)/shard_map/broadcast_in_dim | solution.py:433
  2.0 69.5 %shard_map.85 = (f32[64,2736]{1,0:T(8,128)}, f32[1,16,1024]{2,1,0:T(8,128)}, f32[16,2736]{1,0:T(8,128)}) custom-call(bf16[1024,1024]{1,0:T(8,128)(2,1)} %act_hbm.1, bf16[2736,2048]{1,0:T(8,128)(2,1)} %bitcast.2, f32[1,16,1024]{2,1,0:T(8,128)} %act_hist_ref.1, f32[16,2736]{1,0:T(8,128)} %grad_hist_ref.1, s32[1,1024]{1,0:T(1,128)} %bitcast.3, ...), custom_call_target="tpu_custom_call" | custom-call | tf_op jit(solution)/shard_map/pallas_call | solution.py:394
  71.5 0.0 copy-start
  71.5 1.1 %copy-done = f32[64,2736]{1,0:T(8,128)S(1)} copy-done((f32[64,2736]{1,0:T(8,128)S(1)}, f32[64,2736]{1,0:T(8,128)}, u32[]{:S(2)}) %copy-start) | copy-done | bytes 700440
  72.6 0.0 copy-start.1
  72.6 0.9 %copy-done.1 = f32[16,2736]{1,0:T(8,128)S(1)} copy-done((f32[16,2736]{1,0:T(8,128)S(1)}, f32[16,2736]{1,0:T(8,128)}, u32[]{:S(2)}) %copy-start.1) | copy-done | bytes 175128
  73.6 0.0 copy-start.2
  73.6 0.8 %copy-done.2 = f32[1,16,1024]{2,1,0:T(8,128)S(1)} copy-done((f32[1,16,1024]{2,1,0:T(8,128)S(1)}, f32[1,16,1024]{2,1,0:T(8,128)}, u32[]{:S(2)}) %copy-start.2) | copy-done | bytes 65560
  74.4 1.0 %shard_map.86 = (f32[64,2736]{1,0:T(8,128)}, f32[1,16,1024]{2,1,0:T(8,128)}, f32[16,2736]{1,0:T(8,128)}) custom-call(f32[64,2736]{1,0:T(8,128)S(1)} %copy-done, f32[1,16,1024]{2,1,0:T(8,128)S(1)} %copy-done.2, f32[16,2736]{1,0:T(8,128)S(1)} %copy-done.1), custom_call_target="tpu_custom_call" | custom-call | tf_op jit(solution)/shard_map/pallas_call | solution.py:445
Async XLA Ops:
  71.5 1.1 %copy-start = (f32[64,2736]{1,0:T(8,128)S(1)}, f32[64,2736]{1,0:T(8,128)}, u32[]{:S(2)}) copy-start(f32[64,2736]{1,0:T(8,128)} %get-tuple-element.6.refs_0_) | copy-start | bytes 2101252
  72.6 0.9 %copy-start.1 = (f32[16,2736]{1,0:T(8,128)S(1)}, f32[16,2736]{1,0:T(8,128)}, u32[]{:S(2)}) copy-start(f32[16,2736]{1,0:T(8,128)} %get-tuple-element.8.refs_2_) | copy-start | bytes 525316
  73.6 0.8 %copy-start.2 = (f32[1,16,1024]{2,1,0:T(8,128)S(1)}, f32[1,16,1024]{2,1,0:T(8,128)}, u32[]{:S(2)}) copy-start(f32[1,16,1024]{2,1,0:T(8,128)} %get-tuple-element.7.refs_1_) | copy-start | bytes 196612
where the time goes:
time: 75.7 us; the launch traced here: 75.4 us
  Pallas kernels  70.5 us (93%)
  local copies, waits for them, and re-layouts  4.24 us (6%)
    pallas_call x1, Pallas kernels, fused_outputs(): pl.pallas_call(functools.partial(fused_kernel, dp, tensor), out_shape=(ja...  69.5 us
    unnamed x6, local copies, waits for them, and re-layouts  2.86 us

commit v1 on v0

v1 whole, which is shorter than its diff:
```python
import functools
import math

import jax
import jax.numpy as jnp
from jax import lax
from jax.experimental import pallas as pl
from jax.experimental.pallas import tpu as pltpu
from jax.sharding import PartitionSpec as P

QUANT_LIMIT = 448.0
SCALE_FLOOR = 0.25
CORES = 2
ROWS_Y = 2
LANES = 128
SUBLANES = 16
PIECES = 2
OWN_TILE = 768
GOT_TILE = 1536
TURN = 256
MESH = pl.DeviceIdType.MESH


def quantize(values, scale):
    scaled = values.astype(jnp.float32) * scale
    return jnp.clip(scaled, -QUANT_LIMIT, QUANT_LIMIT).astype(jnp.bfloat16)


def place_peaks(history, peaks, slots):
    rows = lax.broadcasted_iota(jnp.int32, history.shape, 0)
    return jnp.where(rows == slots[None, :], peaks[None, :], history)


def tiles(width, step):
    return [(start, min(step, width - start)) for start in range(0, width, step)]


def fused_kernel(
    dp, tensor,
    act_hbm, grad_hbm, act_hist_hbm, grad_hist_hbm, owner_hbm, slot_hbm,
    weight_ref, act_hist_out, grad_hist_out,
    act_own, act_down, act_got, raw, gq, part, core_got, y_out, y_got, z_out, z_got,
    own_lhs, got_lhs, act_hist, hist_got, grad_hist, owner_ref, slot_ref,
    core_peaks, y_peaks, z_peaks, act_peaks,
    act_scale, scale_down, grad_scale, current_hist,
    load_sem, grad_sem, small_sem, hist_send, hist_recv, pair_send, pair_recv,
    x_send, x_recv, core_send, core_recv, y_send, y_recv, z_send, z_recv,
    pk_send, pk_recv, ap_send, ap_recv,
):
    me = lax.axis_index("dp")
    mt = lax.axis_index("tensor")
    core = lax.rem(me, CORES)
    chip = lax.div(me, CORES)
    yy = lax.rem(chip, ROWS_Y)
    zz = lax.div(chip, ROWS_Y)
    depth = dp // (CORES * ROWS_Y)
    tokens, width = act_hbm.shape
    cols, rows = grad_hbm.shape
    block = width // dp
    piece = block // PIECES
    padded = grad_scale.shape[1]
    full, rest = cols // LANES, cols % LANES
    own_tiles = tiles(padded, OWN_TILE)
    got_tiles = tiles(padded, GOT_TILE)
    steps = ROWS_Y * PIECES

    def dp_index(z, y, c):
        return (z * ROWS_Y + y) * CORES + c

    def on_tensor(t):
        return {"tensor": lax.rem(mt + t, tensor)}

    sibling = {"dp": dp_index(zz, yy, 1 - core)}
    y_peer = {"dp": dp_index(zz, 1 - yy, core)}

    def on_z(k):
        return {"dp": dp_index(lax.rem(zz + k, depth), yy, core)}

    barrier = pltpu.get_barrier_semaphore()
    partners = [on_tensor(t) for t in range(1, tensor)] + [sibling, y_peer]
    partners += [on_z(k) for k in range(1, depth)]
    for partner in partners:
        pl.semaphore_signal(barrier, inc=1, device_id=partner, device_id_type=MESH)

    act_load = pltpu.make_async_copy(act_hbm, act_own, load_sem)
    act_load.start()
    smalls = [
        pltpu.make_async_copy(source, target, small_sem.at[i])
        for i, (source, target) in enumerate((
            (grad_hist_hbm, grad_hist), (act_hist_hbm, act_hist),
            (owner_hbm, owner_ref), (slot_hbm, slot_ref),
        ))
    ]
    for small in smalls:
        small.start()

    def grad_load(i, size=LANES):
        at = pl.ds(i * LANES, size)
        return pltpu.make_async_copy(grad_hbm.at[at], raw.at[at], grad_sem.at[i])

    def start_load(i, carry):
        grad_load(i).start()
        return carry

    lax.fori_loop(0, full, start_load, 0)
    if rest:
        grad_load(full, rest).start()
        raw[cols:, :] = jnp.zeros((padded - cols, rows), jnp.bfloat16)

    def offset_z(u):
        if depth == 4:
            return 2 - u + 3 * lax.div(u, 2) + 2 * lax.div(u, 3)
        return u + 1

    def target_z(u):
        return lax.rem(zz + offset_z(u), depth)

    def side(k):
        return yy * k + (1 - yy) * (1 - k)

    def pair_at(u, k):
        return pl.ds((target_z(u) * ROWS_Y + side(k)) * CORES, CORES)

    def piece_at(s):
        return pl.ds(s * piece, piece)

    def part_rows(k, c, s):
        return pl.ds(
            pl.multiple_of((side(k) * CORES + c) * block + s * piece, piece), piece
        )

    def step_of(u, k, s):
        return u * steps + k * PIECES + s

    def hist_copy(t):
        at = pl.ds(pl.multiple_of(core * (width // CORES), LANES), width // CORES)
        return pltpu.make_async_remote_copy(
            src_ref=act_hist_hbm.at[0, :, at], dst_ref=hist_got.at[t - 1, :, at],
            send_sem=hist_send.at[t - 1], recv_sem=hist_recv.at[t - 1],
            device_id=on_tensor(t), device_id_type=MESH,
        )

    def hist_pass(t):
        at = pl.ds(pl.multiple_of(core * (width // CORES), LANES), width // CORES)
        return pltpu.make_async_remote_copy(
            src_ref=hist_got.at[t - 1, :, at], dst_ref=hist_got.at[t - 1, :, at],
            send_sem=pair_send.at[t - 1], recv_sem=pair_recv.at[t - 1],
            device_id=sibling, device_id_type=MESH,
        )

    def x_copy(t, u, k, s):
        at = step_of(u, k, s)
        return pltpu.make_async_remote_copy(
            src_ref=act_down.at[pair_at(u, k), piece_at(s)],
            dst_ref=act_got.at[t - 1, pair_at(u, k), piece_at(s)],
            send_sem=x_send.at[t - 1, at], recv_sem=x_recv.at[t - 1, at],
            device_id=on_tensor(t), device_id_type=MESH,
        )

    def core_copy(u, k, s, j):
        at = step_of(u, k, s)
        start, size = got_tiles[j]
        return pltpu.make_async_remote_copy(
            src_ref=part.at[u, part_rows(k, 1 - core, s), pl.ds(start, size)],
            dst_ref=core_got.at[at, :, pl.ds(start, size)],
            send_sem=core_send.at[at, j], recv_sem=core_recv.at[at, j],
            device_id=sibling, device_id_type=MESH,
        )

    def y_copy(u, s):
        return pltpu.make_async_remote_copy(
            src_ref=y_out.at[u, piece_at(s)], dst_ref=y_got.at[u, piece_at(s)],
            send_sem=y_send.at[u, s], recv_sem=y_recv.at[u, s],
            device_id=y_peer, device_id_type=MESH,
        )

    def z_copy(u, s):
        return pltpu.make_async_remote_copy(
            src_ref=z_out.at[u, piece_at(s)], dst_ref=z_got.at[u, piece_at(s)],
            send_sem=z_send.at[u, s], recv_sem=z_recv.at[u, s],
            device_id=on_z(offset_z(u)), device_id_type=MESH,
        )

    def peak_copy(buffer, i, partner, at):
        return pltpu.make_async_remote_copy(
            src_ref=buffer.at[0], dst_ref=buffer.at[i],
            send_sem=pk_send.at[at], recv_sem=pk_recv.at[at],
            device_id=partner, device_id_type=MESH,
        )

    core_peak = peak_copy(core_peaks, 1, sibling, 0)
    y_peak = peak_copy(y_peaks, 1, y_peer, 1)
    z_peak = [peak_copy(z_peaks, k, on_z(k), 1 + k) for k in range(1, depth)]

    def act_peak_copy(t):
        return pltpu.make_async_remote_copy(
            src_ref=act_peaks.at[0], dst_ref=act_peaks.at[t],
            send_sem=ap_send.at[t - 1], recv_sem=ap_recv.at[t - 1],
            device_id=on_tensor(t), device_id_type=MESH,
        )

    act_load.wait()

    def turn_act(b, carry):
        at = pl.ds(pl.multiple_of(b * LANES, LANES), LANES)
        read = act_own[:, at]
        top = jnp.max(jnp.abs(read).reshape(tokens // SUBLANES, SUBLANES, LANES), axis=0)
        core_peaks[0, :, at] = jnp.max(top.astype(jnp.float32), axis=0, keepdims=True)
        act_down[pl.ds(b * (LANES // block), LANES // block)] = jnp.transpose(read).reshape(
            LANES // block, block, tokens
        )
        return carry

    lax.fori_loop(0, width // LANES, turn_act, 0)

    pl.semaphore_wait(barrier, len(partners))
    for t in range(1, tensor):
        hist_copy(t).start()

    def send_x(u, carry):
        for k in range(ROWS_Y):
            for s in range(PIECES):
                for t in range(1, tensor):
                    x_copy(t, u, k, s).start()
        return carry

    lax.fori_loop(0, depth, send_x, 0)

    smalls[0].wait()
    if rest:
        grad_scale[:, padded - LANES:] = jnp.ones((1, LANES), jnp.float32)
    grad_scale[:, :cols] = QUANT_LIMIT / jnp.maximum(
        jnp.max(grad_hist[...], axis=0, keepdims=True), SCALE_FLOOR
    )

    def quantize_cols(j):
        at = pl.ds(pl.multiple_of(j * LANES, LANES), LANES)
        scale = grad_scale[:, at]
        top = jnp.zeros((SUBLANES, LANES), jnp.bfloat16)
        for start, size in tiles(rows, TURN):
            turned = jnp.transpose(raw[at, start:start + size])
            mag = jnp.abs(turned).reshape(size // SUBLANES, SUBLANES, LANES)
            top = jnp.maximum(top, jnp.max(mag, axis=0))
            gq[start:start + size, at] = quantize(turned, scale)
        here = pl.ds(pl.multiple_of(width + j * LANES, LANES), LANES)
        core_peaks[0, :, here] = jnp.max(top.astype(jnp.float32), axis=0, keepdims=True)

    def grad_chunk(i, carry):
        grad_load(i).wait()
        quantize_cols(i)
        return carry

    lax.fori_loop(0, full // 2, grad_chunk, 0)
    for t in range(1, tensor):
        hist_copy(t).wait()
        hist_pass(t).start()
    lax.fori_loop(full // 2, full, grad_chunk, 0)
    if rest:
        grad_load(full, rest).wait()
        quantize_cols(full)
    core_peak.start()

    for small in smalls[1:]:
        small.wait()
    owner = owner_ref[...]
    current = jnp.where(owner == mt, act_hist[0], 0.0)
    for t in range(1, tensor):
        hist_pass(t).wait()
        source = lax.rem(mt + tensor - t, tensor)
        current = jnp.where(owner == source, hist_got[t - 1], current)
    current_hist[...] = current
    act_scale[...] = QUANT_LIMIT / jnp.maximum(
        jnp.max(current, axis=0, keepdims=True), SCALE_FLOOR
    )
    for start in range(0, width, LANES):
        turned = jnp.transpose(jnp.broadcast_to(act_scale[:, start:start + LANES], (LANES, LANES)))
        first = start // block
        scale_down[first:first + LANES // block] = turned.reshape(LANES // block, block, LANES)

    def load_own(u):
        at = pl.ds(target_z(u) * (ROWS_Y * CORES), ROWS_Y * CORES)
        count = ROWS_Y * CORES * block
        scale = scale_down[at].reshape(count, LANES)
        for start in range(0, tokens, LANES):
            read = act_down[at, :, start:start + LANES].reshape(count, LANES)
            own_lhs[:, start:start + LANES] = quantize(read, scale)

    def own_product(u, j):
        start, size = own_tiles[j]
        source = pl.ds(pl.multiple_of(mt * tokens, tokens), tokens)
        part[u, :, start:start + size] = jnp.dot(
            own_lhs[...], gq[source, start:start + size], preferred_element_type=jnp.float32
        )

    def got_product(u, k, s):
        scale = scale_down[pair_at(u, k), piece_at(s), :].reshape(CORES * piece, LANES)
        for t in range(1, tensor):
            x_copy(t, u, k, s).wait_recv()
            for start in range(0, tokens, LANES):
                read = act_got[t - 1, pair_at(u, k), piece_at(s), start:start + LANES]
                got_lhs[t - 1, :, start:start + LANES] = quantize(
                    read.reshape(CORES * piece, LANES), scale
                )
        for j, (start, size) in enumerate(got_tiles):
            for t in range(1, tensor):
                from_rank = lax.rem(mt + tensor - t, tensor)
                source = pl.ds(pl.multiple_of(from_rank * tokens, tokens), tokens)
                term = jnp.dot(
                    got_lhs[t - 1], gq[source, start:start + size],
                    preferred_element_type=jnp.float32,
                )
                for c in range(CORES):
                    part[u, part_rows(k, c, s), start:start + size] += term[
                        c * piece:(c + 1) * piece
                    ]
            core_copy(u, k, s, j).start()

    def core_sum(u, k, s, j):
        start, size = got_tiles[j]
        core_copy(u, k, s, j).wait_recv()
        return (
            part[u, part_rows(k, core, s), start:start + size]
            + core_got[step_of(u, k, s), :, start:start + size]
        )

    def send_y(u, s):
        for j, (start, size) in enumerate(got_tiles):
            y_out[u, piece_at(s), start:start + size] = core_sum(u, 0, s, j).astype(jnp.bfloat16)
        y_copy(u, s).start()

    def line_sum(u, s, j):
        start, size = got_tiles[j]
        return core_sum(u, 1, s, j) + y_got[u, piece_at(s), start:start + size].astype(jnp.float32)

    def send_z(u, s):
        y_copy(u, s).wait_recv()
        for j, (start, size) in enumerate(got_tiles):
            z_out[u, piece_at(s), start:start + size] = line_sum(u, s, j).astype(jnp.bfloat16)
        z_copy(u, s).start()

    def unit(u):
        for k in range(ROWS_Y):
            for s in range(PIECES):
                got_product(u, k, s)
                if k == 0 and s == 0:
                    load_own(u + 1)
                for j in range(k * PIECES + s, len(own_tiles), steps):
                    own_product(u + 1, j)
                if k == 0:
                    send_y(u, s)
                else:
                    send_z(u, s)

    load_own(0)
    for j in range(len(own_tiles)):
        own_product(0, j)
    core_peak.wait()
    y_peaks[0] = jnp.max(core_peaks[...], axis=0)
    y_peak.start()

    unit(0)
    y_peak.wait()
    z_peaks[0] = jnp.max(y_peaks[...], axis=0)
    for copy in z_peak:
        copy.start()

    def middle(u, carry):
        unit(u)
        return carry

    lax.fori_loop(1, depth - 1, middle, 0)

    last = depth - 1
    got_product(last, 0, 0)
    for copy in z_peak:
        copy.wait()
    tops = jnp.max(z_peaks[...], axis=0)
    act_peaks[0] = tops[:, :width]
    for t in range(1, tensor):
        act_peak_copy(t).start()
    send_y(last, 0)
    for s in range(1, PIECES):
        got_product(last, 0, s)
        send_y(last, s)

    hist_row = lax.broadcasted_iota(jnp.int32, grad_hist.shape, 0)
    slots = slot_ref[...]
    grad_slots = slots[width:width + cols]
    for t in range(1, tensor):
        first = width + t * cols
        grad_slots = jnp.where(mt == t, slots[first:first + cols], grad_slots)
    grad_hist_out[...] = jnp.where(
        hist_row == grad_slots[None, :], tops[:, width:width + cols], grad_hist[...]
    )
    for t in range(1, tensor):
        act_peak_copy(t).wait()
    hist_row = lax.broadcasted_iota(jnp.int32, current_hist.shape, 0)
    act_hist_out[0] = jnp.where(
        hist_row == slots[:width][None, :], jnp.max(act_peaks[...], axis=0), current_hist[...]
    )
    factor = 1.0 / math.sqrt(rows * dp)
    grad_scale[...] = factor / grad_scale[...]
    undo = 1.0 / scale_down[me]

    for s in range(PIECES):
        got_product(last, 1, s)
        y_copy(last, s).wait_recv()
        for u in range(depth - 1):
            z_copy(u, s).wait_recv()
        for j, (start, size) in enumerate(got_tiles):
            total = line_sum(last, s, j)
            for u in range(depth - 1):
                total = total + z_got[u, piece_at(s), start:start + size].astype(jnp.float32)
            total = total * undo[s * piece:(s + 1) * piece, :1]
            total = total * grad_scale[:, start:start + size]
            size = min(size, cols - start)
            weight_ref[piece_at(s), start:start + size] = total[:, :size]

    def finish(u, carry):
        for s in range(PIECES):
            for k in range(ROWS_Y):
                for t in range(1, tensor):
                    x_copy(t, u, k, s).wait_send()
                for j in range(len(got_tiles)):
                    core_copy(u, k, s, j).wait_send()
            y_copy(u, s).wait_send()
        return carry

    lax.fori_loop(0, depth, finish, 0)

    def finish_z(u, carry):
        for s in range(PIECES):
            z_copy(u, s).wait_send()
        return carry

    lax.fori_loop(0, depth - 1, finish_z, 0)


def fused_outputs(activations, gradients, act_history, grad_history, owner_rank, history_slot):
    dp, tensor = lax.axis_size("dp"), lax.axis_size("tensor")
    tokens, width = activations.shape
    rows, cols = gradients.shape
    hist = act_history.shape[1]
    depth = dp // (CORES * ROWS_Y)
    blocks, block = dp, width // dp
    steps = depth * ROWS_Y * PIECES
    padded = pl.cdiv(cols, LANES) * LANES
    line = ROWS_Y * CORES * block
    dma = pltpu.SemaphoreType.DMA
    vmem = pl.BlockSpec(memory_space=pltpu.VMEM)
    hbm = pl.BlockSpec(memory_space=pl.ANY)
    f32, bf16, i32 = jnp.float32, jnp.bfloat16, jnp.int32
    others = tensor - 1
    halves = len(tiles(padded, GOT_TILE))
    return pl.pallas_call(
        functools.partial(fused_kernel, dp, tensor),
        out_shape=(
            pltpu.VMEM((block, cols), f32),
            pltpu.VMEM((1, hist, width), f32),
            pltpu.VMEM((hist, cols), f32),
        ),
        in_specs=[hbm] * 6,
        out_specs=(vmem, vmem, vmem),
        scratch_shapes=[
            pltpu.VMEM((tokens, width), bf16),
            pltpu.VMEM((blocks, block, tokens), bf16),
            pltpu.VMEM((others, blocks, block, tokens), bf16),
            pltpu.VMEM((padded, rows), bf16),
            pltpu.VMEM((rows, padded), bf16),
            pltpu.VMEM((depth, line, padded), f32),
            pltpu.VMEM((steps, block // PIECES, padded), f32),
            pltpu.VMEM((depth, block, padded), bf16),
            pltpu.VMEM((depth, block, padded), bf16),
            pltpu.VMEM((depth - 1, block, padded), bf16),
            pltpu.VMEM((depth - 1, block, padded), bf16),
            pltpu.VMEM((line, tokens), bf16),
            pltpu.VMEM((others, CORES * (block // PIECES), tokens), bf16),
            pltpu.VMEM((1, hist, width), f32),
            pltpu.VMEM((others, hist, width), f32),
            pltpu.VMEM((hist, cols), f32),
            pltpu.VMEM((1, width), i32),
            pltpu.VMEM(history_slot.shape, i32),
            pltpu.VMEM((2, 1, width + padded), f32),
            pltpu.VMEM((2, 1, width + padded), f32),
            pltpu.VMEM((depth, 1, width + padded), f32),
            pltpu.VMEM((tensor, 1, width), f32),
            pltpu.VMEM((1, width), f32),
            pltpu.VMEM((blocks, block, LANES), f32),
            pltpu.VMEM((1, padded), f32),
            pltpu.VMEM((hist, width), f32),
            dma, dma((padded // LANES,)), dma((4,)), dma((others,)), dma((others,)),
            dma((others,)), dma((others,)),
            dma((others, steps)), dma((others, steps)), dma((steps, halves)), dma((steps, halves)),
            dma((depth, PIECES)), dma((depth, PIECES)), dma((depth - 1, PIECES)), dma((depth - 1, PIECES)),
            dma((depth + 1,)), dma((depth + 1,)), dma((others,)), dma((others,)),
        ],
        compiler_params=pltpu.CompilerParams(
            collective_id=0, has_side_effects=True, vmem_limit_bytes=61 * 1024 * 1024
        ),
    )(
        activations, gradients.T, act_history, grad_history,
        owner_rank[None, :], history_slot,
    )


def hand_over_kernel(*refs):
    sems = refs[-1]
    half = (len(refs) - 1) // 2
    copies = [
        pltpu.make_async_copy(source, target, sems.at[i])
        for i, (source, target) in enumerate(zip(refs[:half], refs[half:-1]))
    ]
    for copy in copies:
        copy.start()
    for copy in copies:
        copy.wait()


def hand_over(*results):
    vmem = pl.BlockSpec(memory_space=pltpu.VMEM)
    hbm = pl.BlockSpec(memory_space=pl.ANY)
    return pl.pallas_call(
        hand_over_kernel,
        out_shape=tuple(jax.ShapeDtypeStruct(r.shape, r.dtype) for r in results),
        in_specs=[vmem] * len(results),
        out_specs=(hbm,) * len(results),
        scratch_shapes=[pltpu.SemaphoreType.DMA((len(results),))],
        compiler_params=pltpu.CompilerParams(vmem_limit_bytes=1024 * 1024),
    )(*results)


def gathered_sums(activations, gradients, act_history, grad_history, owner_rank):
    my_rank = lax.axis_index("tensor")
    held = jnp.where(owner_rank[None, :] == my_rank, act_history[0], jnp.float32(0.0))
    current = lax.psum(held, "tensor")
    act_scale = QUANT_LIMIT / jnp.maximum(jnp.max(current, axis=0), SCALE_FLOOR)
    grad_scale = QUANT_LIMIT / jnp.maximum(jnp.max(grad_history, axis=0), SCALE_FLOOR)
    gathered_rows = lax.all_gather(quantize(activations, act_scale), "tensor", axis=0, tiled=True)
    summed = lax.psum_scatter(
        lax.dot_general(
            gathered_rows, quantize(gradients, grad_scale), (((0,), (0,)), ((), ())),
            preferred_element_type=jnp.float32,
        ),
        "dp", scatter_dimension=0, tiled=True,
    )
    act_peak = lax.pmax(jnp.max(jnp.abs(activations), axis=0).astype(jnp.float32), ("dp", "tensor"))
    grad_peak = lax.pmax(jnp.max(jnp.abs(gradients), axis=0).astype(jnp.float32), "dp")
    return summed, current, act_peak[None, :], grad_peak[None, :]


def body(activations, gradients, act_history, grad_history, owner_rank, history_slot):
    dp = lax.axis_size("dp")
    model_width = act_history.shape[2]
    column_total = gradients.shape[1]
    row_count = model_width // dp
    fits = dp % (CORES * ROWS_Y) == 0 and dp > CORES * ROWS_Y
    fits = fits and LANES % row_count == 0 and row_count % (PIECES * SUBLANES) == 0
    fits = fits and model_width % (CORES * LANES) == 0 and activations.shape[0] % TURN == 0
    fits = fits and column_total % SUBLANES == 0
    if fits:
        return hand_over(*fused_outputs(
            activations, gradients, act_history, grad_history, owner_rank, history_slot
        ))
    act_slots = history_slot[:model_width]
    grad_slots = lax.dynamic_slice_in_dim(
        history_slot, model_width + lax.axis_index("tensor") * column_total, column_total, 0
    )
    summed, current, act_peak, grad_peak = gathered_sums(
        activations, gradients, act_history, grad_history, owner_rank
    )
    act_scale = QUANT_LIMIT / jnp.maximum(jnp.max(current, axis=0), SCALE_FLOOR)
    grad_scale = QUANT_LIMIT / jnp.maximum(jnp.max(grad_history, axis=0), SCALE_FLOOR)
    grad_factor = 1.0 / math.sqrt(gradients.shape[0] * dp)
    row_base = lax.axis_index("dp") * row_count
    row_scale = lax.dynamic_slice_in_dim(act_scale, row_base, row_count, 0)
    weight_grad = summed / (row_scale[:, None] * grad_scale[None, :]) * grad_factor
    act_history_out = place_peaks(current, act_peak[0], act_slots)[None]
    grad_history_out = place_peaks(grad_history, grad_peak[0], grad_slots)
    return (weight_grad, act_history_out, grad_history_out)


def solution(mesh):
    placed = (
        P(("dp", "tensor"), None),
        P("dp", "tensor"),
        P("tensor", None, None),
        P(None, "tensor"),
        P(),
        P(),
    )
    return jax.shard_map(
        body,
        mesh=mesh,
        in_specs=placed,
        out_specs=(P("dp", "tensor"), P("tensor", None, None), P(None, "tensor")),
        check_vma=False,
    )
```

time: 75.7 us -> 67.2 us (0.89)
  Pallas kernels: 70.5 us -> 66.2 us
  local copies, waits for them, and re-layouts: 4.24 us -> 0 us
    pallas_call x1, Pallas kernels: 69.5 us -> 65.3 us  [fused_outputs(): pl.pallas_call(functools.partial(fused_kernel, dp, tensor), out_shape=(pl...]
    unnamed x6 -> x0, local copies, waits for them, and re-layouts: 2.86 us -> none
    broadcast_in_dim x1 -> x0, local copies, waits for them, and re-layouts: 1.37 us -> none  [fused_outputs(): history_slot[None, :]]
where the time goes in v1:
time: 67.2 us; the launch traced here: 67 us
  Pallas kernels  66.2 us (99%)
  between operations  0.8 us (1%)
    pallas_call x1, Pallas kernels, fused_outputs(): pl.pallas_call(functools.partial(fused_kernel, dp, tensor), out_shape=(pl...  65.3 us

profile of v1, /device:TPU:0, one launch (start us, length us, event | category | flops | bytes accessed | tf_op | source)
XLA Modules:
  0.0 67.0 jit_solution(2437184824982538375)
XLA Ops:
  0.6 65.3 %shard_map.85 = (f32[64,2736]{1,0:T(8,128)S(1)}, f32[1,16,1024]{2,1,0:T(8,128)S(1)}, f32[16,2736]{1,0:T(8,128)S(1)}) custom-call(bf16[1024,1024]{1,0:T(8,128)(2,1)} %act_hbm.1, bf16[2736,2048]{1,0:T(8,128)(2,1)} %bitcast.2, f32[1,16,1024]{2,1,0:T(8,128)} %act_hist_hbm.1, f32[16,2736]{1,0:T(8,128)} %grad_hist_hbm.1, s32[1,1024]{1,0:T(1,128)} %bitcast.3, ...), custom_call_target="tpu_custom_call" | custom-call | tf_op jit(solution)/shard_map/pallas_call | solution.py:455
  65.9 1.0 %shard_map.86 = (f32[64,2736]{1,0:T(8,128)}, f32[1,16,1024]{2,1,0:T(8,128)}, f32[16,2736]{1,0:T(8,128)}) custom-call(f32[64,2736]{1,0:T(8,128)S(1)} %get-tuple-element.6.refs_0_, f32[1,16,1024]{2,1,0:T(8,128)S(1)} %get-tuple-element.7.refs_1_, f32[16,2736]{1,0:T(8,128)S(1)} %get-tuple-element.8.refs_2_), custom_call_target="tpu_custom_call" | custom-call | tf_op jit(solution)/shard_map/pallas_call | solution.py:522

commit v2 on v1

v2 whole, which is shorter than its diff:
```python
import functools
import math

import jax
import jax.numpy as jnp
from jax import lax
from jax.experimental import pallas as pl
from jax.experimental.pallas import tpu as pltpu
from jax.sharding import PartitionSpec as P

QUANT_LIMIT = 448.0
SCALE_FLOOR = 0.25
CORES = 2
ROWS_Y = 2
DEPTH = 4
LANES = 128
SUBLANES = 16
PIECES = 2
OWN_TILE = 768
GOT_TILE = 1536
TAIL_CUTS = 2
TURN = 256
MESH = pl.DeviceIdType.MESH


def quantize(values, scale):
    scaled = values.astype(jnp.float32) * scale
    return jnp.clip(scaled, -QUANT_LIMIT, QUANT_LIMIT).astype(jnp.bfloat16)


def place_peaks(history, peaks, slots):
    rows = lax.broadcasted_iota(jnp.int32, history.shape, 0)
    return jnp.where(rows == slots[None, :], peaks[None, :], history)


def tiles(width, step):
    return [(start, min(step, width - start)) for start in range(0, width, step)]


def fused_kernel(
    dp, tensor,
    act_hbm, grad_hbm, act_hist_hbm, grad_hist_hbm, owner_hbm, slot_hbm,
    weight_ref, act_hist_out, grad_hist_out,
    act_own, act_down, act_got, raw, gq, part, core_got, y_out, y_got, z_out, z_got,
    own_lhs, got_lhs, act_hist, hist_got, grad_hist, owner_ref, slot_ref,
    core_peaks, y_peaks, near_peaks, far_peaks, act_peaks,
    act_tops, act_scale, scale_down, grad_scale, grad_undo, far_sem,
    load_sem, grad_sem, small_sem, hist_send, hist_recv, top_send, top_recv,
    x_send, x_recv, core_send, core_recv, y_send, y_recv, z_send, z_recv,
    pk_send, pk_recv, ap_send, ap_recv,
):
    me = lax.axis_index("dp")
    mt = lax.axis_index("tensor")
    core = lax.rem(me, CORES)
    chip = lax.div(me, CORES)
    yy = lax.rem(chip, ROWS_Y)
    zz = lax.div(chip, ROWS_Y)
    depth = DEPTH
    half, odd = lax.div(zz, 2), lax.rem(zz, 2)
    inner = odd * (1 - half) + (1 - odd) * half
    beside = 2 * half + 1 - odd
    tokens, width = act_hbm.shape
    cols, rows = grad_hbm.shape
    block = width // dp
    piece = block // PIECES
    padded = grad_scale.shape[1]
    full, rest = cols // LANES, cols % LANES
    own_tiles = tiles(padded, OWN_TILE)
    got_tiles = tiles(padded, GOT_TILE)
    steps = ROWS_Y * PIECES
    last = depth - 1
    order = [(u, k, s) for u in range(depth) for k in range(ROWS_Y) for s in range(PIECES)]
    at = order.index((last, 0, 0))
    order[at - 1:at + 1] = [order[at], order[at - 1]]

    def dp_index(z, y, c):
        return (z * ROWS_Y + y) * CORES + c

    def on_tensor(t):
        return {"tensor": lax.rem(mt + t, tensor)}

    sibling = {"dp": dp_index(zz, yy, 1 - core)}
    y_peer = {"dp": dp_index(zz, 1 - yy, core)}

    def on_z(z):
        return {"dp": dp_index(z, yy, core)}

    z_near, z_far = on_z(beside), on_z(2 * (1 - half) + odd)

    barrier = pltpu.get_barrier_semaphore()
    partners = [on_tensor(t) for t in range(1, tensor)] + [sibling, y_peer]
    below = lax.div(zz + depth - 1, depth)
    above = 1 - lax.div(zz + 1, depth)

    def greet(semaphore):
        @pl.when(zz > 0)
        def _():
            pl.semaphore_signal(semaphore, inc=1, device_id=on_z(zz - 1), device_id_type=MESH)

        @pl.when(zz < depth - 1)
        def _():
            pl.semaphore_signal(semaphore, inc=1, device_id=on_z(zz + 1), device_id_type=MESH)

    for partner in partners:
        pl.semaphore_signal(barrier, inc=1, device_id=partner, device_id_type=MESH)
    greet(barrier)

    def target_z(u):
        return (3 * (1 - half), 2 - half, beside, zz)[u]

    def side(k):
        return yy * k + (1 - yy) * (1 - k)

    def pair_of(u, k):
        return target_z(u) * ROWS_Y + side(k)

    def pair_at(u, k):
        return pl.ds(pair_of(u, k) * CORES, CORES)

    def pair_cols(u, k):
        return pl.ds(pl.multiple_of(pair_of(u, k) * (CORES * block), LANES), CORES * block)

    def act_load(u, k):
        at = pair_cols(u, k)
        return pltpu.make_async_copy(
            act_hbm.at[:, at], act_own.at[:, at], load_sem.at[u * ROWS_Y + k]
        )

    for u in range(depth):
        for k in range(ROWS_Y):
            act_load(u, k).start()
    smalls = [
        pltpu.make_async_copy(source, target, small_sem.at[i])
        for i, (source, target) in enumerate((
            (grad_hist_hbm, grad_hist), (act_hist_hbm, act_hist),
            (owner_hbm, owner_ref), (slot_hbm, slot_ref),
        ))
    ]
    for small in smalls:
        small.start()

    def grad_load(i, size=LANES):
        at = pl.ds(i * LANES, size)
        return pltpu.make_async_copy(grad_hbm.at[at], raw.at[at], grad_sem.at[i])

    def start_load(i, carry):
        grad_load(i).start()
        return carry

    lax.fori_loop(0, full, start_load, 0)
    if rest:
        grad_load(full, rest).start()
        raw[cols:, :] = jnp.zeros((padded - cols, rows), jnp.bfloat16)

    def piece_at(s):
        return pl.ds(s * piece, piece)

    def part_rows(k, c, s):
        return pl.ds(
            pl.multiple_of((side(k) * CORES + c) * block + s * piece, piece), piece
        )

    def step_of(u, k, s):
        return u * steps + k * PIECES + s

    def hist_copy(t, stage):
        parts = CORES if stage == 2 else CORES * ROWS_Y
        mine = core if stage == 2 else core * ROWS_Y + yy
        at = pl.ds(pl.multiple_of(mine * (width // parts), LANES), width // parts)
        held = hist_got.at[t - 1, :, at]
        return pltpu.make_async_remote_copy(
            src_ref=held if stage else act_hist_hbm.at[0, :, at], dst_ref=held,
            send_sem=hist_send.at[t - 1, stage], recv_sem=hist_recv.at[t - 1, stage],
            device_id=(on_tensor(t), y_peer, sibling)[stage], device_id_type=MESH,
        )

    def top_copy(t):
        return pltpu.make_async_remote_copy(
            src_ref=act_tops.at[0], dst_ref=act_tops.at[t],
            send_sem=top_send.at[t - 1], recv_sem=top_recv.at[t - 1],
            device_id=on_tensor(t), device_id_type=MESH,
        )

    def pass_hist(stage):
        for t in range(1, tensor):
            hist_copy(t, stage - 1).wait()
            if stage < 3:
                hist_copy(t, stage).start()

    def x_copy(t, u, k, s, cut=0, cuts=1):
        at = step_of(u, k, s) + cut
        span = pl.ds(cut * (tokens // cuts), tokens // cuts)
        return pltpu.make_async_remote_copy(
            src_ref=act_down.at[pair_at(u, k), piece_at(s), span],
            dst_ref=act_got.at[t - 1, pair_at(u, k), piece_at(s), span],
            send_sem=x_send.at[t - 1, at], recv_sem=x_recv.at[t - 1, at],
            device_id=on_tensor(t), device_id_type=MESH,
        )

    def core_copy(u, k, s, j):
        at = step_of(u, k, s)
        start, size = got_tiles[j]
        return pltpu.make_async_remote_copy(
            src_ref=part.at[u, part_rows(k, 1 - core, s), pl.ds(start, size)],
            dst_ref=core_got.at[at, :, pl.ds(start, size)],
            send_sem=core_send.at[at, j], recv_sem=core_recv.at[at, j],
            device_id=sibling, device_id_type=MESH,
        )

    def y_copy(u, s, j):
        at = pl.ds(*got_tiles[j])
        return pltpu.make_async_remote_copy(
            src_ref=y_out.at[u, piece_at(s), at], dst_ref=y_got.at[u, piece_at(s), at],
            send_sem=y_send.at[u, s, j], recv_sem=y_recv.at[u, s, j],
            device_id=y_peer, device_id_type=MESH,
        )

    def z_copy(u, s, j, slot=None):
        at = pl.ds(*got_tiles[j])
        goal, into = beside, u
        if u < 2:
            goal = inner * target_z(u) + (1 - inner) * beside
            into = inner * last + (1 - inner) * u
        into = into if slot is None else slot
        return pltpu.make_async_remote_copy(
            src_ref=z_out.at[u, piece_at(s), at], dst_ref=z_got.at[into, piece_at(s), at],
            send_sem=z_send.at[u, s, j], recv_sem=z_recv.at[into, s, j],
            device_id=on_z(goal), device_id_type=MESH,
        )

    def peak_copy(buffer, i, partner, at):
        return pltpu.make_async_remote_copy(
            src_ref=buffer.at[0], dst_ref=buffer.at[i],
            send_sem=pk_send.at[at], recv_sem=pk_recv.at[at],
            device_id=partner, device_id_type=MESH,
        )

    core_peak = peak_copy(core_peaks, 1, sibling, 0)
    y_peak = peak_copy(y_peaks, 1, y_peer, 1)
    near_peak = peak_copy(near_peaks, 1, z_near, 2)
    far_peak = peak_copy(far_peaks, 1, z_far, 3)

    def act_peak_copy(t):
        return pltpu.make_async_remote_copy(
            src_ref=act_peaks.at[0], dst_ref=act_peaks.at[t],
            send_sem=ap_send.at[t - 1], recv_sem=ap_recv.at[t - 1],
            device_id=on_tensor(t), device_id_type=MESH,
        )

    def turn_act(u, k):
        act_load(u, k).wait()
        at = pair_cols(u, k)
        read = act_own[:, at]
        top = jnp.max(jnp.abs(read).reshape(tokens // SUBLANES, SUBLANES, CORES * block), axis=0)
        core_peaks[0, :, at] = jnp.max(top.astype(jnp.float32), axis=0, keepdims=True)
        act_down[pair_at(u, k)] = jnp.transpose(read).reshape(CORES, block, tokens)

    def send_x(u, k, s, cuts=1):
        for t in range(1, tensor):
            for cut in range(cuts):
                x_copy(t, u, k, s, cut, cuts).start()

    turn_act(*order[0][:2])
    pl.semaphore_wait(barrier, len(partners) + below + above)
    greet(far_sem)
    smalls[1].wait()
    act_tops[0] = jnp.max(act_hist[0], axis=0, keepdims=True)
    for t in range(1, tensor):
        top_copy(t).start()
    turned = {order[0][:2]}
    for u, k, s in order:
        if (u, k) not in turned:
            turn_act(u, k)
            turned.add((u, k))
        send_x(u, k, s, TAIL_CUTS if (u, k, s) == order[-1] else 1)
        if (u, k, s) == order[1]:
            for t in range(1, tensor):
                hist_copy(t, 0).start()

    smalls[0].wait()
    if rest:
        grad_scale[:, padded - LANES:] = jnp.ones((1, LANES), jnp.float32)
    grad_scale[:, :cols] = QUANT_LIMIT / jnp.maximum(
        jnp.max(grad_hist[...], axis=0, keepdims=True), SCALE_FLOOR
    )

    def quantize_cols(j):
        at = pl.ds(pl.multiple_of(j * LANES, LANES), LANES)
        scale = grad_scale[:, at]
        top = jnp.zeros((SUBLANES, LANES), jnp.bfloat16)
        for start, size in tiles(rows, TURN):
            turned = jnp.transpose(raw[at, start:start + size])
            mag = jnp.abs(turned).reshape(size // SUBLANES, SUBLANES, LANES)
            top = jnp.maximum(top, jnp.max(mag, axis=0))
            gq[start:start + size, at] = quantize(turned, scale)
        here = pl.ds(pl.multiple_of(width + j * LANES, LANES), LANES)
        core_peaks[0, :, here] = jnp.max(top.astype(jnp.float32), axis=0, keepdims=True)

    def grad_chunk(i, carry):
        grad_load(i).wait()
        quantize_cols(i)
        return carry

    lax.fori_loop(0, full, grad_chunk, 0)
    if rest:
        grad_load(full, rest).wait()
        quantize_cols(full)
    core_peak.start()
    pl.semaphore_wait(far_sem, below + above)

    smalls[2].wait()
    owner = owner_ref[...]
    top = act_tops[0]
    for t in range(1, tensor):
        top_copy(t).wait()
        top = jnp.where(owner == lax.rem(mt + tensor - t, tensor), act_tops[t], top)
    act_scale[...] = QUANT_LIMIT / jnp.maximum(top, SCALE_FLOOR)
    for start in range(0, width, LANES):
        turned = jnp.transpose(jnp.broadcast_to(act_scale[:, start:start + LANES], (LANES, LANES)))
        first = start // block
        scale_down[first:first + LANES // block] = turned.reshape(LANES // block, block, LANES)

    def load_own(u):
        at = pl.ds(target_z(u) * (ROWS_Y * CORES), ROWS_Y * CORES)
        count = ROWS_Y * CORES * block
        scale = scale_down[at].reshape(count, LANES)
        for start in range(0, tokens, LANES):
            read = act_down[at, :, start:start + LANES].reshape(count, LANES)
            own_lhs[:, start:start + LANES] = quantize(read, scale)

    def own_product(u, j):
        start, size = own_tiles[j]
        source = pl.ds(pl.multiple_of(mt * tokens, tokens), tokens)
        part[u, :, start:start + size] = jnp.dot(
            own_lhs[...], gq[source, start:start + size], preferred_element_type=jnp.float32
        )

    def got_product(u, k, s, cuts=1):
        scale = scale_down[pair_at(u, k), piece_at(s), :].reshape(CORES * piece, LANES)
        span = tokens // cuts
        for cut in range(cuts):
            first = cut * span
            for t in range(1, tensor):
                x_copy(t, u, k, s, cut, cuts).wait_recv()
                for start in range(first, first + span, LANES):
                    read = act_got[t - 1, pair_at(u, k), piece_at(s), start:start + LANES]
                    got_lhs[t - 1, :, start:start + LANES] = quantize(
                        read.reshape(CORES * piece, LANES), scale
                    )
            for j, (start, size) in enumerate(got_tiles):
                for t in range(1, tensor):
                    from_rank = lax.rem(mt + tensor - t, tensor)
                    source = pl.ds(pl.multiple_of(from_rank * tokens + first, TURN), span)
                    term = jnp.dot(
                        got_lhs[t - 1, :, first:first + span], gq[source, start:start + size],
                        preferred_element_type=jnp.float32,
                    )
                    for c in range(CORES):
                        part[u, part_rows(k, c, s), start:start + size] += term[
                            c * piece:(c + 1) * piece
                        ]
                if cut == cuts - 1:
                    core_copy(u, k, s, j).start()

    def core_sum(u, k, s, j):
        start, size = got_tiles[j]
        core_copy(u, k, s, j).wait_recv()
        return (
            part[u, part_rows(k, core, s), start:start + size]
            + core_got[step_of(u, k, s), :, start:start + size]
        )

    def send_y(u, s):
        for j, (start, size) in enumerate(got_tiles):
            y_out[u, piece_at(s), start:start + size] = core_sum(u, 0, s, j).astype(jnp.bfloat16)
            y_copy(u, s, j).start()

    def line_sum(u, s, j):
        start, size = got_tiles[j]
        return core_sum(u, 1, s, j) + y_got[u, piece_at(s), start:start + size].astype(jnp.float32)

    def send_z(u, s, add):
        for j, (start, size) in enumerate(got_tiles):
            y_copy(u, s, j).wait_recv()
            total = line_sum(u, s, j)
            if add:
                z_copy(u, s, j, u).wait_recv()
                total = total + z_got[u, piece_at(s), start:start + size].astype(jnp.float32)
            z_out[u, piece_at(s), start:start + size] = total.astype(jnp.bfloat16)
            z_copy(u, s, j).start()

    load_own(0)
    for j in range(len(own_tiles)):
        own_product(0, j)
    core_peak.wait()
    y_peaks[0] = jnp.max(core_peaks[...], axis=0)
    y_peak.start()

    def finish_line(s):
        for j, (start, size) in enumerate(got_tiles):
            y_copy(last, s, j).wait_recv()
            for u in (2, last):
                z_copy(2, s, j, u).wait_recv()
            total = line_sum(last, s, j)
            for u in (2, last):
                total = total + z_got[u, piece_at(s), start:start + size].astype(jnp.float32)
            total = total * undo[s * piece:(s + 1) * piece, :1]
            total = total * grad_undo[:, start:start + size]
            size = min(size, cols - start)
            weight_ref[piece_at(s), start:start + size] = total[:, :size]

    where = {step: i for i, step in enumerate(order)}
    fillers, sends = [[] for _ in order], [[] for _ in order]
    far_sends = [[], []]
    for u in range(last):
        first, until = where[u, 0, 0], where[u + 1, 0, 0]
        for j in range(len(own_tiles)):
            fillers[min(first + j, until - 1)].append((u + 1, j))
        for s in range(PIECES):
            if u < 2:
                far_sends[0].append((where[u, 1, s] + 2 - u, u, s))
                far_sends[1].append((where[u, 1, s] + 5 - 2 * u, u, s))
            else:
                sends[where[u, 1, s] + 1 - s].append((1, u, s))
    for u in range(depth):
        for s in range(PIECES):
            sends[where[u, 0, s] + (1 if u == 0 else 0)].append((0, u, s))
    for i, (u, k, s) in enumerate(order):
        got_product(u, k, s, TAIL_CUTS if i == len(order) - 1 else 1)
        if u < last and (u, k, s) == (u, 0, 0):
            load_own(u + 1)
        for other, j in fillers[i]:
            own_product(other, j)
        for add, plan in enumerate(far_sends):
            due = [(other, piece_of) for at, other, piece_of in plan if at == i]

            @pl.when(inner == add)
            def _(due=due, add=add):
                for other, piece_of in due:
                    send_z(other, piece_of, add)

        for kind, other, piece_of in sends[i]:
            if kind == 0:
                send_y(other, piece_of)
            else:
                send_z(other, piece_of, 0)
        if i == steps - 1:
            y_peak.wait()
            near_peaks[0] = jnp.max(y_peaks[...], axis=0)
            near_peak.start()
            pass_hist(1)
        if i == steps + 1:
            near_peak.wait()
            far_peaks[0] = jnp.max(near_peaks[...], axis=0)
            far_peak.start()
            pass_hist(2)
        if i == where[last, 0, PIECES - 1]:
            far_peak.wait()
            tops = jnp.max(far_peaks[...], axis=0)
            act_peaks[0] = tops[:, :width]
            for t in range(1, tensor):
                act_peak_copy(t).start()
            factor = 1.0 / math.sqrt(rows * dp)
            grad_undo[...] = factor / grad_scale[...]
            undo = 1.0 / scale_down[me]
            pass_hist(3)
            smalls[3].wait()
            slots = slot_ref[...]
            hist_row = lax.broadcasted_iota(jnp.int32, grad_hist.shape, 0)
            grad_slots = slots[width:width + cols]
            for t in range(1, tensor):
                first = width + t * cols
                grad_slots = jnp.where(mt == t, slots[first:first + cols], grad_slots)
            grad_hist_out[...] = jnp.where(
                hist_row == grad_slots[None, :], tops[:, width:width + cols], grad_hist[...]
            )
        if i == len(order) - 1:
            for t in range(1, tensor):
                act_peak_copy(t).wait()
            current = act_hist[0]
            for t in range(1, tensor):
                source = lax.rem(mt + tensor - t, tensor)
                current = jnp.where(owner_ref[...] == source, hist_got[t - 1], current)
            hist_row = lax.broadcasted_iota(jnp.int32, current.shape, 0)
            act_hist_out[0] = jnp.where(
                hist_row == slots[:width][None, :], jnp.max(act_peaks[...], axis=0), current
            )
            for piece_of in range(PIECES):
                finish_line(piece_of)

    for u, k, s in order:
        for t in range(1, tensor):
            cuts = TAIL_CUTS if (u, k, s) == order[-1] else 1
            for cut in range(cuts):
                x_copy(t, u, k, s, cut, cuts).wait_send()
        for j in range(len(got_tiles)):
            core_copy(u, k, s, j).wait_send()
            if k == 0:
                y_copy(u, s, j).wait_send()
            elif u < last:
                z_copy(u, s, j).wait_send()


def fused_outputs(activations, gradients, act_history, grad_history, owner_rank, history_slot):
    dp, tensor = lax.axis_size("dp"), lax.axis_size("tensor")
    tokens, width = activations.shape
    rows, cols = gradients.shape
    hist = act_history.shape[1]
    depth = dp // (CORES * ROWS_Y)
    blocks, block = dp, width // dp
    steps = depth * ROWS_Y * PIECES
    pieces = steps + TAIL_CUTS - 1
    padded = pl.cdiv(cols, LANES) * LANES
    line = ROWS_Y * CORES * block
    dma = pltpu.SemaphoreType.DMA
    vmem = pl.BlockSpec(memory_space=pltpu.VMEM)
    hbm = pl.BlockSpec(memory_space=pl.ANY)
    f32, bf16, i32 = jnp.float32, jnp.bfloat16, jnp.int32
    others = tensor - 1
    halves = len(tiles(padded, GOT_TILE))
    return pl.pallas_call(
        functools.partial(fused_kernel, dp, tensor),
        out_shape=(
            pltpu.VMEM((block, cols), f32),
            pltpu.VMEM((1, hist, width), f32),
            pltpu.VMEM((hist, cols), f32),
        ),
        in_specs=[hbm] * 6,
        out_specs=(vmem, vmem, vmem),
        scratch_shapes=[
            pltpu.VMEM((tokens, width), bf16),
            pltpu.VMEM((blocks, block, tokens), bf16),
            pltpu.VMEM((others, blocks, block, tokens), bf16),
            pltpu.VMEM((padded, rows), bf16),
            pltpu.VMEM((rows, padded), bf16),
            pltpu.VMEM((depth, line, padded), f32),
            pltpu.VMEM((steps, block // PIECES, padded), f32),
            pltpu.VMEM((depth, block, padded), bf16),
            pltpu.VMEM((depth, block, padded), bf16),
            pltpu.VMEM((depth - 1, block, padded), bf16),
            pltpu.VMEM((depth, block, padded), bf16),
            pltpu.VMEM((line, tokens), bf16),
            pltpu.VMEM((others, CORES * (block // PIECES), tokens), bf16),
            pltpu.VMEM((1, hist, width), f32),
            pltpu.VMEM((others, hist, width), f32),
            pltpu.VMEM((hist, cols), f32),
            pltpu.VMEM((1, width), i32),
            pltpu.VMEM(history_slot.shape, i32),
            pltpu.VMEM((2, 1, width + padded), f32),
            pltpu.VMEM((2, 1, width + padded), f32),
            pltpu.VMEM((2, 1, width + padded), f32),
            pltpu.VMEM((2, 1, width + padded), f32),
            pltpu.VMEM((tensor, 1, width), f32),
            pltpu.VMEM((tensor, 1, width), f32),
            pltpu.VMEM((1, width), f32),
            pltpu.VMEM((blocks, block, LANES), f32),
            pltpu.VMEM((1, padded), f32),
            pltpu.VMEM((1, padded), f32),
            pltpu.SemaphoreType.REGULAR,
            dma((depth * ROWS_Y,)), dma((padded // LANES,)), dma((4,)), dma((others, 3)), dma((others, 3)), dma((others,)), dma((others,)),
            dma((others, pieces)), dma((others, pieces)), dma((steps, halves)), dma((steps, halves)),
            dma((depth, PIECES, halves)), dma((depth, PIECES, halves)),
            dma((depth - 1, PIECES, halves)), dma((depth, PIECES, halves)),
            dma((4,)), dma((4,)), dma((others,)), dma((others,)),
        ],
        compiler_params=pltpu.CompilerParams(
            collective_id=0, has_side_effects=True, vmem_limit_bytes=61 * 1024 * 1024
        ),
    )(
        activations, gradients.T, act_history, grad_history,
        owner_rank[None, :], history_slot,
    )


def hand_over_kernel(*refs):
    sems = refs[-1]
    half = (len(refs) - 1) // 2
    copies = [
        pltpu.make_async_copy(source, target, sems.at[i])
        for i, (source, target) in enumerate(zip(refs[:half], refs[half:-1]))
    ]
    for copy in copies:
        copy.start()
    for copy in copies:
        copy.wait()


def hand_over(*results):
    vmem = pl.BlockSpec(memory_space=pltpu.VMEM)
    hbm = pl.BlockSpec(memory_space=pl.ANY)
    return pl.pallas_call(
        hand_over_kernel,
        out_shape=tuple(jax.ShapeDtypeStruct(r.shape, r.dtype) for r in results),
        in_specs=[vmem] * len(results),
        out_specs=(hbm,) * len(results),
        scratch_shapes=[pltpu.SemaphoreType.DMA((len(results),))],
        compiler_params=pltpu.CompilerParams(vmem_limit_bytes=1024 * 1024),
    )(*results)


def gathered_sums(activations, gradients, act_history, grad_history, owner_rank):
    my_rank = lax.axis_index("tensor")
    held = jnp.where(owner_rank[None, :] == my_rank, act_history[0], jnp.float32(0.0))
    current = lax.psum(held, "tensor")
    act_scale = QUANT_LIMIT / jnp.maximum(jnp.max(current, axis=0), SCALE_FLOOR)
    grad_scale = QUANT_LIMIT / jnp.maximum(jnp.max(grad_history, axis=0), SCALE_FLOOR)
    gathered_rows = lax.all_gather(quantize(activations, act_scale), "tensor", axis=0, tiled=True)
    summed = lax.psum_scatter(
        lax.dot_general(
            gathered_rows, quantize(gradients, grad_scale), (((0,), (0,)), ((), ())),
            preferred_element_type=jnp.float32,
        ),
        "dp", scatter_dimension=0, tiled=True,
    )
    act_peak = lax.pmax(jnp.max(jnp.abs(activations), axis=0).astype(jnp.float32), ("dp", "tensor"))
    grad_peak = lax.pmax(jnp.max(jnp.abs(gradients), axis=0).astype(jnp.float32), "dp")
    return summed, current, act_peak[None, :], grad_peak[None, :]


def body(activations, gradients, act_history, grad_history, owner_rank, history_slot):
    dp = lax.axis_size("dp")
    model_width = act_history.shape[2]
    column_total = gradients.shape[1]
    row_count = model_width // dp
    fits = dp == CORES * ROWS_Y * DEPTH
    fits = fits and (row_count * CORES) % LANES == 0 and row_count % (PIECES * SUBLANES) == 0
    fits = fits and model_width % (CORES * ROWS_Y * LANES) == 0 and activations.shape[0] % (TAIL_CUTS * TURN) == 0
    fits = fits and column_total % SUBLANES == 0
    if fits:
        return hand_over(*fused_outputs(
            activations, gradients, act_history, grad_history, owner_rank, history_slot
        ))
    act_slots = history_slot[:model_width]
    grad_slots = lax.dynamic_slice_in_dim(
        history_slot, model_width + lax.axis_index("tensor") * column_total, column_total, 0
    )
    summed, current, act_peak, grad_peak = gathered_sums(
        activations, gradients, act_history, grad_history, owner_rank
    )
    act_scale = QUANT_LIMIT / jnp.maximum(jnp.max(current, axis=0), SCALE_FLOOR)
    grad_scale = QUANT_LIMIT / jnp.maximum(jnp.max(grad_history, axis=0), SCALE_FLOOR)
    grad_factor = 1.0 / math.sqrt(gradients.shape[0] * dp)
    row_base = lax.axis_index("dp") * row_count
    row_scale = lax.dynamic_slice_in_dim(act_scale, row_base, row_count, 0)
    weight_grad = summed / (row_scale[:, None] * grad_scale[None, :]) * grad_factor
    act_history_out = place_peaks(current, act_peak[0], act_slots)[None]
    grad_history_out = place_peaks(grad_history, grad_peak[0], grad_slots)
    return (weight_grad, act_history_out, grad_history_out)


def solution(mesh):
    placed = (
        P(("dp", "tensor"), None),
        P("dp", "tensor"),
        P("tensor", None, None),
        P(None, "tensor"),
        P(),
        P(),
    )
    return jax.shard_map(
        body,
        mesh=mesh,
        in_specs=placed,
        out_specs=(P("dp", "tensor"), P("tensor", None, None), P(None, "tensor")),
        check_vma=False,
    )
```

time: 67.2 us -> 58.3 us (0.87)
  Pallas kernels: 66.2 us -> 57.3 us
    pallas_call x1, Pallas kernels: 65.3 us -> 56.4 us  [fused_outputs(): pl.pallas_call(functools.partial(fused_kernel, dp, tensor), out_shape=(pl...]
where the time goes in v2:
time: 58.3 us; the launch traced here: 58.2 us
  Pallas kernels  57.3 us (98%)
  between operations  0.82 us (1%)
    pallas_call x1, Pallas kernels, fused_outputs(): pl.pallas_call(functools.partial(fused_kernel, dp, tensor), out_shape=(pl...  56.4 us

profile of v2, /device:TPU:0, one launch (start us, length us, event | category | flops | bytes accessed | tf_op | source)
XLA Modules:
  0.0 58.2 jit_solution(2395535473146849168)
XLA Ops:
  0.6 56.4 %shard_map.85 = (f32[64,2736]{1,0:T(8,128)S(1)}, f32[1,16,1024]{2,1,0:T(8,128)S(1)}, f32[16,2736]{1,0:T(8,128)S(1)}) custom-call(bf16[1024,1024]{1,0:T(8,128)(2,1)} %act_hbm.1, bf16[2736,2048]{1,0:T(8,128)(2,1)} %bitcast.2, f32[1,16,1024]{2,1,0:T(8,128)} %act_hist_hbm.1, f32[16,2736]{1,0:T(8,128)} %grad_hist_hbm.1, s32[1,1024]{1,0:T(1,128)} %bitcast.3, ...), custom_call_target="tpu_custom_call" | custom-call | tf_op jit(solution)/shard_map/pallas_call | solution.py:521
  57.0 1.0 %shard_map.86 = (f32[64,2736]{1,0:T(8,128)}, f32[1,16,1024]{2,1,0:T(8,128)}, f32[16,2736]{1,0:T(8,128)}) custom-call(f32[64,2736]{1,0:T(8,128)S(1)} %get-tuple-element.6.refs_0_, f32[1,16,1024]{2,1,0:T(8,128)S(1)} %get-tuple-element.7.refs_1_, f32[16,2736]{1,0:T(8,128)S(1)} %get-tuple-element.8.refs_2_), custom_call_target="tpu_custom_call" | custom-call | tf_op jit(solution)/shard_map/pallas_call | solution.py:591

commit v3 on v2

--- a/solution.py
+++ b/solution.py
@@ -19,6 +19,8 @@
 OWN_TILE = 768
 GOT_TILE = 1536
 TAIL_CUTS = 2
+RING = 8
+GROUP = 3
 TURN = 256
 MESH = pl.DeviceIdType.MESH
 
@@ -35,6 +37,19 @@
 
 def tiles(width, step):
     return [(start, min(step, width - start)) for start in range(0, width, step)]
+
+
+def piece_plan(block):
+    size = block // PIECES
+    fine = size // 2
+    spans = [(i * size, size) for i in range(PIECES)]
+    order = [[(u, k, s)] for u in range(DEPTH) for k in range(ROWS_Y) for s in spans]
+    last = DEPTH - 1
+    at = order.index([(last, 0, spans[0])])
+    cuts = [(block - size + i * fine, fine) for i in range(2)]
+    order[at - 1] = order[at]
+    order[at:at + 2] = [[(last, 0, cut), (last - 1, 1, cut)] for cut in cuts]
+    return spans, cuts, order
 
 
 def fused_kernel(
@@ -64,14 +79,13 @@
     block = width // dp
     piece = block // PIECES
     padded = grad_scale.shape[1]
-    full, rest = cols // LANES, cols % LANES
     own_tiles = tiles(padded, OWN_TILE)
     got_tiles = tiles(padded, GOT_TILE)
     steps = ROWS_Y * PIECES
     last = depth - 1
-    order = [(u, k, s) for u in range(depth) for k in range(ROWS_Y) for s in range(PIECES)]
-    at = order.index((last, 0, 0))
-    order[at - 1:at + 1] = [order[at], order[at - 1]]
+    spans, cut_spans, order = piece_plan(block)
+    number = {step: i for i, step in enumerate(step for group in order for step in group)}
+    last_spans = spans[:-1] + cut_spans
 
     def dp_index(z, y, c):
         return (z * ROWS_Y + y) * CORES + c
@@ -123,8 +137,12 @@
     def act_load(u, k):
         at = pair_cols(u, k)
         return pltpu.make_async_copy(
-            act_hbm.at[:, at], act_own.at[:, at], load_sem.at[u * ROWS_Y + k]
-        )
+            act_hbm.at[:, at], act_own.at[:, at], load_sem.at[min(u * ROWS_Y + k, 1)]
+        )
+
+    def act_rest():
+        at = pl.ds(0, width - CORES * block)
+        return pltpu.make_async_copy(act_hbm.at[:, at], act_own.at[:, at], load_sem.at[1])
 
     for u in range(depth):
         for k in range(ROWS_Y):
@@ -139,29 +157,28 @@
     for small in smalls:
         small.start()
 
-    def grad_load(i, size=LANES):
-        at = pl.ds(i * LANES, size)
+    group = GROUP * LANES
+    groups, rest = cols // group, cols % group
+
+    def grad_load(i, size=group):
+        at = pl.ds(i * group, size)
         return pltpu.make_async_copy(grad_hbm.at[at], raw.at[at], grad_sem.at[i])
 
     def start_load(i, carry):
         grad_load(i).start()
         return carry
 
-    lax.fori_loop(0, full, start_load, 0)
+    lax.fori_loop(0, groups, start_load, 0)
     if rest:
-        grad_load(full, rest).start()
+        grad_load(groups, rest).start()
+    if padded > cols:
         raw[cols:, :] = jnp.zeros((padded - cols, rows), jnp.bfloat16)
 
     def piece_at(s):
-        return pl.ds(s * piece, piece)
+        return pl.ds(*s)
 
     def part_rows(k, c, s):
-        return pl.ds(
-            pl.multiple_of((side(k) * CORES + c) * block + s * piece, piece), piece
-        )
-
-    def step_of(u, k, s):
-        return u * steps + k * PIECES + s
+        return pl.ds(pl.multiple_of((side(k) * CORES + c) * block + s[0], s[1]), s[1])
 
     def hist_copy(t, stage):
         parts = CORES if stage == 2 else CORES * ROWS_Y
@@ -170,7 +187,7 @@
         held = hist_got.at[t - 1, :, at]
         return pltpu.make_async_remote_copy(
             src_ref=held if stage else act_hist_hbm.at[0, :, at], dst_ref=held,
-            send_sem=hist_send.at[t - 1, stage], recv_sem=hist_recv.at[t - 1, stage],
+            send_sem=hist_send.at[t - 1], recv_sem=hist_recv.at[t - 1, stage],
             device_id=(on_tensor(t), y_peer, sibling)[stage], device_id_type=MESH,
         )
 
@@ -188,50 +205,59 @@
                 hist_copy(t, stage).start()
 
     def x_copy(t, u, k, s, cut=0, cuts=1):
-        at = step_of(u, k, s) + cut
+        at = number[u, k, s] + cut
         span = pl.ds(cut * (tokens // cuts), tokens // cuts)
         return pltpu.make_async_remote_copy(
             src_ref=act_down.at[pair_at(u, k), piece_at(s), span],
             dst_ref=act_got.at[t - 1, pair_at(u, k), piece_at(s), span],
-            send_sem=x_send.at[t - 1, at], recv_sem=x_recv.at[t - 1, at],
+            send_sem=x_send.at[t - 1], recv_sem=x_recv.at[t - 1, at],
             device_id=on_tensor(t), device_id_type=MESH,
         )
 
     def core_copy(u, k, s, j):
-        at = step_of(u, k, s)
+        at = number[u, k, s]
         start, size = got_tiles[j]
         return pltpu.make_async_remote_copy(
             src_ref=part.at[u, part_rows(k, 1 - core, s), pl.ds(start, size)],
-            dst_ref=core_got.at[at, :, pl.ds(start, size)],
-            send_sem=core_send.at[at, j], recv_sem=core_recv.at[at, j],
+            dst_ref=core_got.at[at, pl.ds(0, s[1]), pl.ds(start, size)],
+            send_sem=core_send, recv_sem=core_recv.at[at % RING, j],
             device_id=sibling, device_id_type=MESH,
         )
 
-    def y_copy(u, s, j):
-        at = pl.ds(*got_tiles[j])
+    whole = [(0, padded)]
+
+    def y_copy(u, s, j=0):
+        at = pl.ds(*(got_tiles if u == last else whole)[j])
+        index = u * PIECES + spans.index(s) if u < last else (
+            last * PIECES + last_spans.index(s) * len(got_tiles) + j
+        )
         return pltpu.make_async_remote_copy(
             src_ref=y_out.at[u, piece_at(s), at], dst_ref=y_got.at[u, piece_at(s), at],
-            send_sem=y_send.at[u, s, j], recv_sem=y_recv.at[u, s, j],
+            send_sem=y_send, recv_sem=y_recv.at[index],
             device_id=y_peer, device_id_type=MESH,
         )
 
-    def z_copy(u, s, j, slot=None):
-        at = pl.ds(*got_tiles[j])
-        goal, into = beside, u
+    def z_copy(u, s, j=0, slot=None):
+        at = pl.ds(*(got_tiles if u == 2 else whole)[j])
+        goal, into, index = beside, u, last * PIECES + j
         if u < 2:
             goal = inner * target_z(u) + (1 - inner) * beside
             into = inner * last + (1 - inner) * u
-        into = into if slot is None else slot
+            into = into if slot is None else slot
+            index = (inner * 2 + (1 - inner) * u if slot is None else min(slot, 2)) * PIECES
+            index = index + spans.index(s)
+        else:
+            index += last_spans.index(s) * len(got_tiles)
         return pltpu.make_async_remote_copy(
             src_ref=z_out.at[u, piece_at(s), at], dst_ref=z_got.at[into, piece_at(s), at],
-            send_sem=z_send.at[u, s, j], recv_sem=z_recv.at[into, s, j],
+            send_sem=z_send, recv_sem=z_recv.at[index],
             device_id=on_z(goal), device_id_type=MESH,
         )
 
     def peak_copy(buffer, i, partner, at):
         return pltpu.make_async_remote_copy(
             src_ref=buffer.at[0], dst_ref=buffer.at[i],
-            send_sem=pk_send.at[at], recv_sem=pk_recv.at[at],
+            send_sem=pk_send, recv_sem=pk_recv.at[at],
             device_id=partner, device_id_type=MESH,
         )
 
@@ -248,7 +274,6 @@
         )
 
     def turn_act(u, k):
-        act_load(u, k).wait()
         at = pair_cols(u, k)
         read = act_own[:, at]
         top = jnp.max(jnp.abs(read).reshape(tokens // SUBLANES, SUBLANES, CORES * block), axis=0)
@@ -260,25 +285,28 @@
             for cut in range(cuts):
                 x_copy(t, u, k, s, cut, cuts).start()
 
-    turn_act(*order[0][:2])
+    act_load(0, 0).wait()
+    turn_act(0, 0)
     pl.semaphore_wait(barrier, len(partners) + below + above)
     greet(far_sem)
     smalls[1].wait()
     act_tops[0] = jnp.max(act_hist[0], axis=0, keepdims=True)
     for t in range(1, tensor):
         top_copy(t).start()
-    turned = {order[0][:2]}
-    for u, k, s in order:
+    turned = {(0, 0)}
+    for u, k, s in number:
         if (u, k) not in turned:
+            if len(turned) == 1:
+                act_rest().wait()
             turn_act(u, k)
             turned.add((u, k))
-        send_x(u, k, s, TAIL_CUTS if (u, k, s) == order[-1] else 1)
-        if (u, k, s) == order[1]:
+        send_x(u, k, s, TAIL_CUTS if number[u, k, s] == len(number) - 1 else 1)
+        if number[u, k, s] == 1:
             for t in range(1, tensor):
                 hist_copy(t, 0).start()
 
     smalls[0].wait()
-    if rest:
+    if padded > cols:
         grad_scale[:, padded - LANES:] = jnp.ones((1, LANES), jnp.float32)
     grad_scale[:, :cols] = QUANT_LIMIT / jnp.maximum(
         jnp.max(grad_hist[...], axis=0, keepdims=True), SCALE_FLOOR
@@ -298,13 +326,15 @@
 
     def grad_chunk(i, carry):
         grad_load(i).wait()
-        quantize_cols(i)
+        for j in range(GROUP):
+            quantize_cols(i * GROUP + j)
         return carry
 
-    lax.fori_loop(0, full, grad_chunk, 0)
+    lax.fori_loop(0, groups, grad_chunk, 0)
     if rest:
-        grad_load(full, rest).wait()
-        quantize_cols(full)
+        grad_load(groups, rest).wait()
+        for j in range(pl.cdiv(rest, LANES)):
+            quantize_cols(groups * GROUP + j)
     core_peak.start()
     pl.semaphore_wait(far_sem, below + above)
 
@@ -335,59 +365,70 @@
             own_lhs[...], gq[source, start:start + size], preferred_element_type=jnp.float32
         )
 
-    def got_product(u, k, s, cuts=1):
-        scale = scale_down[pair_at(u, k), piece_at(s), :].reshape(CORES * piece, LANES)
+    def got_product(group, cuts=1):
         span = tokens // cuts
+        places, total = [], 0
+        for u, k, s in group:
+            places.append((u, k, s, total))
+            total += CORES * s[1]
         for cut in range(cuts):
             first = cut * span
-            for t in range(1, tensor):
-                x_copy(t, u, k, s, cut, cuts).wait_recv()
-                for start in range(first, first + span, LANES):
-                    read = act_got[t - 1, pair_at(u, k), piece_at(s), start:start + LANES]
-                    got_lhs[t - 1, :, start:start + LANES] = quantize(
-                        read.reshape(CORES * piece, LANES), scale
-                    )
+            for u, k, s, base in places:
+                count = CORES * s[1]
+                scale = scale_down[pair_at(u, k), piece_at(s), :].reshape(count, LANES)
+                for t in range(1, tensor):
+                    x_copy(t, u, k, s, cut, cuts).wait_recv()
+                    for start in range(first, first + span, LANES):
+                        read = act_got[t - 1, pair_at(u, k), piece_at(s), start:start + LANES]
+                        got_lhs[t - 1, base:base + count, start:start + LANES] = quantize(
+                            read.reshape(count, LANES), scale
+                        )
             for j, (start, size) in enumerate(got_tiles):
                 for t in range(1, tensor):
                     from_rank = lax.rem(mt + tensor - t, tensor)
                     source = pl.ds(pl.multiple_of(from_rank * tokens + first, TURN), span)
                     term = jnp.dot(
-                        got_lhs[t - 1, :, first:first + span], gq[source, start:start + size],
-                        preferred_element_type=jnp.float32,
+                        got_lhs[t - 1, :total, first:first + span],
+                        gq[source, start:start + size], preferred_element_type=jnp.float32,
                     )
-                    for c in range(CORES):
-                        part[u, part_rows(k, c, s), start:start + size] += term[
-                            c * piece:(c + 1) * piece
-                        ]
+                    for u, k, s, base in places:
+                        for c in range(CORES):
+                            at = base + c * s[1]
+                            part[u, part_rows(k, c, s), start:start + size] += term[at:at + s[1]]
                 if cut == cuts - 1:
-                    core_copy(u, k, s, j).start()
+                    for u, k, s in group:
+                        core_copy(u, k, s, j).start()
 
     def core_sum(u, k, s, j):
         start, size = got_tiles[j]
         core_copy(u, k, s, j).wait_recv()
         return (
             part[u, part_rows(k, core, s), start:start + size]
-            + core_got[step_of(u, k, s), :, start:start + size]
+            + core_got[number[u, k, s], :s[1], start:start + size]
         )
 
     def send_y(u, s):
         for j, (start, size) in enumerate(got_tiles):
             y_out[u, piece_at(s), start:start + size] = core_sum(u, 0, s, j).astype(jnp.bfloat16)
-            y_copy(u, s, j).start()
+            if u == last or j == len(got_tiles) - 1:
+                y_copy(u, s, j if u == last else 0).start()
 
     def line_sum(u, s, j):
         start, size = got_tiles[j]
         return core_sum(u, 1, s, j) + y_got[u, piece_at(s), start:start + size].astype(jnp.float32)
 
     def send_z(u, s, add):
+        if u < last - 1 or s != cut_spans[1]:
+            y_copy(u, spans[s[0] // piece]).wait_recv()
+        if add:
+            z_copy(u, s, 0, u).wait_recv()
         for j, (start, size) in enumerate(got_tiles):
-            y_copy(u, s, j).wait_recv()
             total = line_sum(u, s, j)
             if add:
-                z_copy(u, s, j, u).wait_recv()
                 total = total + z_got[u, piece_at(s), start:start + size].astype(jnp.float32)
             z_out[u, piece_at(s), start:start + size] = total.astype(jnp.bfloat16)
-            z_copy(u, s, j).start()
+            if u == 2 or j == len(got_tiles) - 1:
+                z_copy(u, s, j if u == 2 else 0).start()
 
     load_own(0)
     for j in range(len(own_tiles)):
@@ -397,38 +438,40 @@
     y_peak.start()
 
     def finish_line(s):
+        z_copy(0, s, 0, last).wait_recv()
         for j, (start, size) in enumerate(got_tiles):
-            y_copy(last, s, j).wait_recv()
-            for u in (2, last):
-                z_copy(2, s, j, u).wait_recv()
+            for part_of in last_spans:
+                if s[0] <= part_of[0] < s[0] + s[1]:
+                    z_copy(last - 1, part_of, j).wait_recv()
+                    y_copy(last, part_of, j).wait_recv()
             total = line_sum(last, s, j)
             for u in (2, last):
                 total = total + z_got[u, piece_at(s), start:start + size].astype(jnp.float32)
-            total = total * undo[s * piece:(s + 1) * piece, :1]
+            total = total * undo[s[0]:s[0] + s[1], :1]
             total = total * grad_undo[:, start:start + size]
             size = min(size, cols - start)
             weight_ref[piece_at(s), start:start + size] = total[:, :size]
 
-    where = {step: i for i, step in enumerate(order)}
+    where = {step: i for i, group in enumerate(order) for step in group}
     fillers, sends = [[] for _ in order], [[] for _ in order]
     far_sends = [[], []]
+    for u, k, s in number:
+        i = where[u, k, s]
+        if k == 0:
+            sends[i + (1 if u == 0 else 0)].append((0, u, s))
+        elif u < 2:
+            far_sends[0].append((i + 2 - u, u, s))
+            far_sends[1].append((i + 5 - 2 * u, u, s))
+        elif u == 2:
+            sends[i if s in cut_spans else i + 1].append((1, u, s))
+    starts = [where[u, 0, spans[0]] for u in range(depth)]
     for u in range(last):
-        first, until = where[u, 0, 0], where[u + 1, 0, 0]
         for j in range(len(own_tiles)):
-            fillers[min(first + j, until - 1)].append((u + 1, j))
-        for s in range(PIECES):
-            if u < 2:
-                far_sends[0].append((where[u, 1, s] + 2 - u, u, s))
-                far_sends[1].append((where[u, 1, s] + 5 - 2 * u, u, s))
-            else:
-                sends[where[u, 1, s] + 1 - s].append((1, u, s))
-    for u in range(depth):
-        for s in range(PIECES):
-            sends[where[u, 0, s] + (1 if u == 0 else 0)].append((0, u, s))
-    for i, (u, k, s) in enumerate(order):
-        got_product(u, k, s, TAIL_CUTS if i == len(order) - 1 else 1)
-        if u < last and (u, k, s) == (u, 0, 0):
-            load_own(u + 1)
+            fillers[min(starts[u] + j, starts[u + 1] - 1)].append((u + 1, j))
+    for i, group in enumerate(order):
+        got_product(group, TAIL_CUTS if i == len(order) - 1 else 1)
+        if i in starts[:last]:
+            load_own(starts.index(i) + 1)
         for other, j in fillers[i]:
             own_product(other, j)
         for add, plan in enumerate(far_sends):
@@ -454,7 +497,7 @@
             far_peaks[0] = jnp.max(near_peaks[...], axis=0)
             far_peak.start()
             pass_hist(2)
-        if i == where[last, 0, PIECES - 1]:
+        if i == where[last, 0, cut_spans[1]]:
             far_peak.wait()
             tops = jnp.max(far_peaks[...], axis=0)
             act_peaks[0] = tops[:, :width]
@@ -485,20 +528,20 @@
             act_hist_out[0] = jnp.where(
                 hist_row == slots[:width][None, :], jnp.max(act_peaks[...], axis=0), current
             )
-            for piece_of in range(PIECES):
-                finish_line(piece_of)
-
-    for u, k, s in order:
-        for t in range(1, tensor):
-            cuts = TAIL_CUTS if (u, k, s) == order[-1] else 1
-            for cut in range(cuts):
-                x_copy(t, u, k, s, cut, cuts).wait_send()
-        for j in range(len(got_tiles)):
-            core_copy(u, k, s, j).wait_send()
-            if k == 0:
-                y_copy(u, s, j).wait_send()
-            elif u < last:
-                z_copy(u, s, j).wait_send()
+            for span in spans:
+                finish_line(span)
+
+    def all_sent(held, semaphore):
+        pltpu.make_async_remote_copy(
+            src_ref=held, dst_ref=held, send_sem=semaphore, recv_sem=semaphore,
+            device_id=sibling, device_id_type=MESH,
+        ).wait_send()
+
+    for t in range(1, tensor):
+        all_sent(act_down, x_send.at[t - 1])
+    all_sent(part.at[pl.ds(0, depth // CORES)], core_send)
+    all_sent(y_out, y_send)
+    all_sent(z_out, z_send)
 
 
 def fused_outputs(activations, gradients, act_history, grad_history, owner_rank, history_slot):
@@ -508,8 +551,9 @@
     hist = act_history.shape[1]
     depth = dp // (CORES * ROWS_Y)
     blocks, block = dp, width // dp
-    steps = depth * ROWS_Y * PIECES
+    steps = sum(len(group) for group in piece_plan(block)[2])
     pieces = steps + TAIL_CUTS - 1
+    hops = (depth - 1) * PIECES + (PIECES + 1) * len(tiles(pl.cdiv(cols, LANES) * LANES, GOT_TILE))
     padded = pl.cdiv(cols, LANES) * LANES
     line = ROWS_Y * CORES * block
     dma = pltpu.SemaphoreType.DMA
@@ -518,6 +562,7 @@
     f32, bf16, i32 = jnp.float32, jnp.bfloat16, jnp.int32
     others = tensor - 1
     halves = len(tiles(padded, GOT_TILE))
+    loads = pl.cdiv(cols, GROUP * LANES)
     return pl.pallas_call(
         functools.partial(fused_kernel, dp, tensor),
         out_shape=(
@@ -557,11 +602,11 @@
             pltpu.VMEM((1, padded), f32),
             pltpu.VMEM((1, padded), f32),
             pltpu.SemaphoreType.REGULAR,
-            dma((depth * ROWS_Y,)), dma((padded // LANES,)), dma((4,)), dma((others, 3)), dma((others, 3)), dma((others,)), dma((others,)),
-            dma((others, pieces)), dma((others, pieces)), dma((steps, halves)), dma((steps, halves)),
-            dma((depth, PIECES, halves)), dma((depth, PIECES, halves)),
-            dma((depth - 1, PIECES, halves)), dma((depth, PIECES, halves)),
-            dma((4,)), dma((4,)), dma((others,)), dma((others,)),
+            dma((2,)), dma((loads,)), dma((4,)),
+            dma((others,)), dma((others, 3)), dma((others,)), dma((others,)),
+            dma((others,)), dma((others, pieces)), dma, dma((RING, halves)),
+            dma, dma((hops,)), dma, dma((hops,)),
+            dma, dma((4,)), dma((others,)), dma((others,)),
         ],
         compiler_params=pltpu.CompilerParams(
             collective_id=0, has_side_effects=True, vmem_limit_bytes=61 * 1024 * 1024
@@ -623,7 +668,7 @@
     column_total = gradients.shape[1]
     row_count = model_width // dp
     fits = dp == CORES * ROWS_Y * DEPTH
-    fits = fits and (row_count * CORES) % LANES == 0 and row_count % (PIECES * SUBLANES) == 0
+    fits = fits and (row_count * CORES) % LANES == 0 and row_count % (PIECES * 2 * SUBLANES) == 0
     fits = fits and model_width % (CORES * ROWS_Y * LANES) == 0 and activations.shape[0] % (TAIL_CUTS * TURN) == 0
     fits = fits and column_total % SUBLANES == 0
     if fits:

time: 58.3 us -> 55.7 us (0.955)
  Pallas kernels: 57.3 us -> 54.8 us
    pallas_call x1, Pallas kernels: 56.4 us -> 53.8 us  [fused_outputs(): pl.pallas_call(functools.partial(fused_kernel, dp, tensor), out_shape=(pl...]
where the time goes in v3:
time: 55.7 us; the launch traced here: 55.6 us
  Pallas kernels  54.8 us (98%)
  between operations  0.82 us (1%)
    pallas_call x1, Pallas kernels, fused_outputs(): pl.pallas_call(functools.partial(fused_kernel, dp, tensor), out_shape=(pl...  53.8 us

profile of v3, /device:TPU:0, one launch (start us, length us, event | category | flops | bytes accessed | tf_op | source)
XLA Modules:
  0.0 55.6 jit_solution(14139800333220919997)
XLA Ops:
  0.6 53.8 %shard_map.85 = (f32[64,2736]{1,0:T(8,128)S(1)}, f32[1,16,1024]{2,1,0:T(8,128)S(1)}, f32[16,2736]{1,0:T(8,128)S(1)}) custom-call(bf16[1024,1024]{1,0:T(8,128)(2,1)} %act_hbm.1, bf16[2736,2048]{1,0:T(8,128)(2,1)} %bitcast.2, f32[1,16,1024]{2,1,0:T(8,128)} %act_hist_hbm.1, f32[16,2736]{1,0:T(8,128)} %grad_hist_hbm.1, s32[1,1024]{1,0:T(1,128)} %bitcast.3, ...), custom_call_target="tpu_custom_call" | custom-call | tf_op jit(solution)/shard_map/pallas_call | solution.py:566
  54.4 1.0 %shard_map.86 = (f32[64,2736]{1,0:T(8,128)}, f32[1,16,1024]{2,1,0:T(8,128)}, f32[16,2736]{1,0:T(8,128)}) custom-call(f32[64,2736]{1,0:T(8,128)S(1)} %get-tuple-element.6.refs_0_, f32[1,16,1024]{2,1,0:T(8,128)S(1)} %get-tuple-element.7.refs_1_, f32[16,2736]{1,0:T(8,128)S(1)} %get-tuple-element.8.refs_2_), custom_call_target="tpu_custom_call" | custom-call | tf_op jit(solution)/shard_map/pallas_call | solution.py:636

commit v4 on v3

--- a/solution.py
+++ b/solution.py
@@ -19,6 +19,7 @@
 OWN_TILE = 768
 GOT_TILE = 1536
 TAIL_CUTS = 2
+TAIL_STEPS = 2
 RING = 8
 GROUP = 3
 TURN = 256
@@ -50,6 +51,16 @@
     order[at - 1] = order[at]
     order[at:at + 2] = [[(last, 0, cut), (last - 1, 1, cut)] for cut in cuts]
     return spans, cuts, order
+
+
+def x_plan(order):
+    slots, cuts_at, free = {}, [], 0
+    for i, group in enumerate(order):
+        cuts_at.append(TAIL_CUTS if i >= len(order) - TAIL_STEPS else 1)
+        for step in group:
+            slots[step] = free
+            free += cuts_at[-1]
+    return slots, cuts_at
 
 
 def fused_kernel(
@@ -86,6 +97,7 @@
     spans, cut_spans, order = piece_plan(block)
     number = {step: i for i, step in enumerate(step for group in order for step in group)}
     last_spans = spans[:-1] + cut_spans
+    x_slots, cuts_at = x_plan(order)
 
     def dp_index(z, y, c):
         return (z * ROWS_Y + y) * CORES + c
@@ -157,11 +169,11 @@
     for small in smalls:
         small.start()
 
-    group = GROUP * LANES
-    groups, rest = cols // group, cols % group
-
-    def grad_load(i, size=group):
-        at = pl.ds(i * group, size)
+    wide = GROUP * LANES
+    groups, rest = cols // wide, cols % wide
+
+    def grad_load(i, size=wide):
+        at = pl.ds(i * wide, size)
         return pltpu.make_async_copy(grad_hbm.at[at], raw.at[at], grad_sem.at[i])
 
     def start_load(i, carry):
@@ -205,7 +217,7 @@
                 hist_copy(t, stage).start()
 
     def x_copy(t, u, k, s, cut=0, cuts=1):
-        at = number[u, k, s] + cut
+        at = x_slots[u, k, s] + cut
         span = pl.ds(cut * (tokens // cuts), tokens // cuts)
         return pltpu.make_async_remote_copy(
             src_ref=act_down.at[pair_at(u, k), piece_at(s), span],
@@ -280,10 +292,11 @@
         core_peaks[0, :, at] = jnp.max(top.astype(jnp.float32), axis=0, keepdims=True)
         act_down[pair_at(u, k)] = jnp.transpose(read).reshape(CORES, block, tokens)
 
-    def send_x(u, k, s, cuts=1):
-        for t in range(1, tensor):
-            for cut in range(cuts):
-                x_copy(t, u, k, s, cut, cuts).start()
+    def send_x(group, cuts):
+        for cut in range(cuts):
+            for u, k, s in group:
+                for t in range(1, tensor):
+                    x_copy(t, u, k, s, cut, cuts).start()
 
     act_load(0, 0).wait()
     turn_act(0, 0)
@@ -294,14 +307,15 @@
     for t in range(1, tensor):
         top_copy(t).start()
     turned = {(0, 0)}
-    for u, k, s in number:
-        if (u, k) not in turned:
-            if len(turned) == 1:
-                act_rest().wait()
-            turn_act(u, k)
-            turned.add((u, k))
-        send_x(u, k, s, TAIL_CUTS if number[u, k, s] == len(number) - 1 else 1)
-        if number[u, k, s] == 1:
+    for i, group in enumerate(order):
+        for u, k, s in group:
+            if (u, k) not in turned:
+                if len(turned) == 1:
+                    act_rest().wait()
+                turn_act(u, k)
+                turned.add((u, k))
+        send_x(group, cuts_at[i])
+        if i == 1:
             for t in range(1, tensor):
                 hist_copy(t, 0).start()
 
@@ -365,7 +379,7 @@
             own_lhs[...], gq[source, start:start + size], preferred_element_type=jnp.float32
         )
 
-    def got_product(group, cuts=1):
+    def got_product(group, cuts):
         span = tokens // cuts
         places, total = [], 0
         for u, k, s in group:
@@ -407,28 +421,28 @@
             + core_got[number[u, k, s], :s[1], start:start + size]
         )
 
-    def send_y(u, s):
-        for j, (start, size) in enumerate(got_tiles):
-            y_out[u, piece_at(s), start:start + size] = core_sum(u, 0, s, j).astype(jnp.bfloat16)
-            if u == last or j == len(got_tiles) - 1:
-                y_copy(u, s, j if u == last else 0).start()
+    def send_y(u, s, j):
+        start, size = got_tiles[j]
+        y_out[u, piece_at(s), start:start + size] = core_sum(u, 0, s, j).astype(jnp.bfloat16)
+        if u == last or j == len(got_tiles) - 1:
+            y_copy(u, s, j if u == last else 0).start()
 
     def line_sum(u, s, j):
         start, size = got_tiles[j]
         return core_sum(u, 1, s, j) + y_got[u, piece_at(s), start:start + size].astype(jnp.float32)
 
-    def send_z(u, s, add):
-        if u < last - 1 or s != cut_spans[1]:
+    def send_z(u, s, add, j):
+        start, size = got_tiles[j]
+        if j == 0 and (u < last - 1 or s != cut_spans[1]):
             y_copy(u, spans[s[0] // piece]).wait_recv()
+        if j == 0 and add:
+            z_copy(u, s, 0, u).wait_recv()
+        total = line_sum(u, s, j)
         if add:
-            z_copy(u, s, 0, u).wait_recv()
-        for j, (start, size) in enumerate(got_tiles):
-            total = line_sum(u, s, j)
-            if add:
-                total = total + z_got[u, piece_at(s), start:start + size].astype(jnp.float32)
-            z_out[u, piece_at(s), start:start + size] = total.astype(jnp.bfloat16)
-            if u == 2 or j == len(got_tiles) - 1:
-                z_copy(u, s, j if u == 2 else 0).start()
+            total = total + z_got[u, piece_at(s), start:start + size].astype(jnp.float32)
+        z_out[u, piece_at(s), start:start + size] = total.astype(jnp.bfloat16)
+        if u == 2 or j == len(got_tiles) - 1:
+            z_copy(u, s, j if u == 2 else 0).start()
 
     load_own(0)
     for j in range(len(own_tiles)):
@@ -469,7 +483,7 @@
         for j in range(len(own_tiles)):
             fillers[min(starts[u] + j, starts[u + 1] - 1)].append((u + 1, j))
     for i, group in enumerate(order):
-        got_product(group, TAIL_CUTS if i == len(order) - 1 else 1)
+        got_product(group, cuts_at[i])
         if i in starts[:last]:
             load_own(starts.index(i) + 1)
         for other, j in fillers[i]:
@@ -480,13 +494,15 @@
             @pl.when(inner == add)
             def _(due=due, add=add):
                 for other, piece_of in due:
-                    send_z(other, piece_of, add)
-
-        for kind, other, piece_of in sends[i]:
-            if kind == 0:
-                send_y(other, piece_of)
-            else:
-                send_z(other, piece_of, 0)
+                    for j in range(len(got_tiles)):
+                        send_z(other, piece_of, add, j)
+
+        for j in range(len(got_tiles)):
+            for kind, other, piece_of in sends[i]:
+                if kind == 0:
+                    send_y(other, piece_of, j)
+                else:
+                    send_z(other, piece_of, 0, j)
         if i == steps - 1:
             y_peak.wait()
             near_peaks[0] = jnp.max(y_peaks[...], axis=0)
@@ -551,8 +567,10 @@
     hist = act_history.shape[1]
     depth = dp // (CORES * ROWS_Y)
     blocks, block = dp, width // dp
-    steps = sum(len(group) for group in piece_plan(block)[2])
-    pieces = steps + TAIL_CUTS - 1
+    order = piece_plan(block)[2]
+    steps = sum(len(group) for group in order)
+    slots, cuts_at = x_plan(order)
+    pieces = max(slots.values()) + cuts_at[-1]
     hops = (depth - 1) * PIECES + (PIECES + 1) * len(tiles(pl.cdiv(cols, LANES) * LANES, GOT_TILE))
     padded = pl.cdiv(cols, LANES) * LANES
     line = ROWS_Y * CORES * block

time: 55.7 us -> 55.3 us (level)
  no operation moved by 1% of the time
where the time goes in v4:
time: 55.3 us; the launch traced here: 55.2 us
  Pallas kernels  54.4 us (98%)
  between operations  0.82 us (1%)
    pallas_call x1, Pallas kernels, fused_outputs(): pl.pallas_call(functools.partial(fused_kernel, dp, tensor), out_shape=(pl...  53.4 us

profile of v4, /device:TPU:0, one launch (start us, length us, event | category | flops | bytes accessed | tf_op | source)
XLA Modules:
  0.0 55.2 jit_solution(2788176799982927334)
XLA Ops:
  0.6 53.4 %shard_map.85 = (f32[64,2736]{1,0:T(8,128)S(1)}, f32[1,16,1024]{2,1,0:T(8,128)S(1)}, f32[16,2736]{1,0:T(8,128)S(1)}) custom-call(bf16[1024,1024]{1,0:T(8,128)(2,1)} %act_hbm.1, bf16[2736,2048]{1,0:T(8,128)(2,1)} %bitcast.2, f32[1,16,1024]{2,1,0:T(8,128)} %act_hist_hbm.1, f32[16,2736]{1,0:T(8,128)} %grad_hist_hbm.1, s32[1,1024]{1,0:T(1,128)} %bitcast.3, ...), custom_call_target="tpu_custom_call" | custom-call | tf_op jit(solution)/shard_map/pallas_call | solution.py:584
  54.0 1.0 %shard_map.86 = (f32[64,2736]{1,0:T(8,128)}, f32[1,16,1024]{2,1,0:T(8,128)}, f32[16,2736]{1,0:T(8,128)}) custom-call(f32[64,2736]{1,0:T(8,128)S(1)} %get-tuple-element.6.refs_0_, f32[1,16,1024]{2,1,0:T(8,128)S(1)} %get-tuple-element.7.refs_1_, f32[16,2736]{1,0:T(8,128)S(1)} %get-tuple-element.8.refs_2_), custom_call_target="tpu_custom_call" | custom-call | tf_op jit(solution)/shard_map/pallas_call | solution.py:654

commit v5 on v4

--- a/solution.py
+++ b/solution.py
@@ -19,7 +19,7 @@
 OWN_TILE = 768
 GOT_TILE = 1536
 TAIL_CUTS = 2
-TAIL_STEPS = 2
+TAIL_STEPS = 1
 RING = 8
 GROUP = 3
 TURN = 256
@@ -50,6 +50,7 @@
     cuts = [(block - size + i * fine, fine) for i in range(2)]
     order[at - 1] = order[at]
     order[at:at + 2] = [[(last, 0, cut), (last - 1, 1, cut)] for cut in cuts]
+    order[at + 2:] = [[(last, 1, s) for s in spans]]
     return spans, cuts, order
 
 
@@ -603,7 +604,7 @@
             pltpu.VMEM((depth - 1, block, padded), bf16),
             pltpu.VMEM((depth, block, padded), bf16),
             pltpu.VMEM((line, tokens), bf16),
-            pltpu.VMEM((others, CORES * (block // PIECES), tokens), bf16),
+            pltpu.VMEM((others, CORES * block, tokens), bf16),
             pltpu.VMEM((1, hist, width), f32),
             pltpu.VMEM((others, hist, width), f32),
             pltpu.VMEM((hist, cols), f32),

time: 55.3 us -> 55.7 us (level)
  no operation moved by 1% of the time
where the time goes in v5:
time: 55.7 us; the launch traced here: 55.5 us
  Pallas kernels  54.7 us (98%)
  between operations  0.82 us (1%)
    pallas_call x1, Pallas kernels, fused_outputs(): pl.pallas_call(functools.partial(fused_kernel, dp, tensor), out_shape=(pl...  53.7 us

profile of v5, /device:TPU:0, one launch (start us, length us, event | category | flops | bytes accessed | tf_op | source)
XLA Modules:
  0.0 55.5 jit_solution(333975732576495438)
XLA Ops:
  0.6 53.7 %shard_map.85 = (f32[64,2736]{1,0:T(8,128)S(1)}, f32[1,16,1024]{2,1,0:T(8,128)S(1)}, f32[16,2736]{1,0:T(8,128)S(1)}) custom-call(bf16[1024,1024]{1,0:T(8,128)(2,1)} %act_hbm.1, bf16[2736,2048]{1,0:T(8,128)(2,1)} %bitcast.2, f32[1,16,1024]{2,1,0:T(8,128)} %act_hist_hbm.1, f32[16,2736]{1,0:T(8,128)} %grad_hist_hbm.1, s32[1,1024]{1,0:T(1,128)} %bitcast.3, ...), custom_call_target="tpu_custom_call" | custom-call | tf_op jit(solution)/shard_map/pallas_call | solution.py:585
  54.4 1.0 %shard_map.86 = (f32[64,2736]{1,0:T(8,128)}, f32[1,16,1024]{2,1,0:T(8,128)}, f32[16,2736]{1,0:T(8,128)}) custom-call(f32[64,2736]{1,0:T(8,128)S(1)} %get-tuple-element.6.refs_0_, f32[1,16,1024]{2,1,0:T(8,128)S(1)} %get-tuple-element.7.refs_1_, f32[16,2736]{1,0:T(8,128)S(1)} %get-tuple-element.8.refs_2_), custom_call_target="tpu_custom_call" | custom-call | tf_op jit(solution)/shard_map/pallas_call | solution.py:655
